TPU v7x, 32 devices: a whole 2x2x4 slice. The times are simulated.
32 devices in a mesh: rep: 2 (over x), dp: 16 (over y, z, core).
Axes of the slice: x: 2, y: 2, z: 4, core: 2. Of those that a mesh axis runs over, the one named last changes fastest.
Arguments:
- x: bfloat16 [32, 2048, 1024], P(('rep', 'dp')), parts along dimension 0
- dy: bfloat16 [32, 2048, 1024], P(('rep', 'dp')), parts along dimension 0
- w_gate: bfloat16 [2, 1024, 4096], replicated
- w_up: bfloat16 [2, 1024, 4096], replicated
- w_down: bfloat16 [2, 4096, 1024], replicated
- m_w_gate: float32 [2, 1024, 4096], P(None, 'dp')
- m_w_up: float32 [2, 1024, 4096], P(None, 'dp')
- m_w_down: float32 [2, 4096, 1024], P(None, 'dp')
- v_w_gate: float32 [2, 1024, 4096], P(None, 'dp')
- v_w_up: float32 [2, 1024, 4096], P(None, 'dp')
- v_w_down: float32 [2, 4096, 1024], P(None, 'dp')
Outputs:
- output 1: bfloat16 [4, 1024, 4096], P('rep'), parts along dimension 0
- output 2: bfloat16 [4, 1024, 4096], P('rep'), parts along dimension 0
- output 3: bfloat16 [4, 4096, 1024], P('rep'), parts along dimension 0
- output 4: float32 [4, 1024, 4096], P('rep', 'dp'), parts along dimension 0
- output 5: float32 [4, 1024, 4096], P('rep', 'dp'), parts along dimension 0
- output 6: float32 [4, 4096, 1024], P('rep', 'dp'), parts along dimension 0
- output 7: float32 [4, 1024, 4096], P('rep', 'dp'), parts along dimension 0
- output 8: float32 [4, 1024, 4096], P('rep', 'dp'), parts along dimension 0
- output 9: float32 [4, 4096, 1024], P('rep', 'dp'), parts along dimension 0
There are 2 independent parts. A program takes and returns all parts, laid end to end along the dimension named above; an argument that names none is the same for every part.
All inputs are finite; a program needn't handle non-finite values.
Results may differ from a plain program's by a relative error of at most 0.022.
Values are sent between devices in bfloat16 or wider.
A program may use at most 2 GiB of HBM per device.

v0:
```python
import jax
import jax.numpy as jnp
from jax import lax

NAMES = ("w_gate", "w_up", "w_down")


def matmul(a, w):
    return jnp.dot(a, w, preferred_element_type=jnp.float32).astype(jnp.bfloat16)


def normed(h):
    wide = h.astype(jnp.float32)
    scale = lax.rsqrt(jnp.mean(wide**2, -1, keepdims=True) + 1e-6)
    return (wide * scale).astype(jnp.bfloat16)


def layer(h, w):
    a = normed(h)
    gate = jnp.dot(a, w["w_gate"], preferred_element_type=jnp.float32)
    up = jnp.dot(a, w["w_up"], preferred_element_type=jnp.float32)
    return h + matmul((jax.nn.silu(gate) * up).astype(jnp.bfloat16), w["w_down"])


def adamw(w, m, v, g):
    m = 0.9 * m + 0.1 * g
    v = 0.95 * v + 0.05 * g * g
    step = m * lax.rsqrt(v + 1e-8) + 0.1 * w
    return (w - 0.02 * step).astype(jnp.bfloat16), m, v


def clipped(gradients, sum_of_squares, count):
    factor = jnp.minimum(1.0, 0.5 * lax.rsqrt(sum_of_squares / count + 1e-30))
    return [g * factor for g in gradients]


def stack(weights, h):
    for number in range(weights["w_gate"].shape[0]):
        h = layer(h, {name: w[number] for name, w in weights.items()})
    return h


def solution(mesh):
    groups = mesh.shape["rep"]

    def step(x, dy, *arrays):
        weights, m, v = (arrays[i : i + 3] for i in (0, 3, 6))
        x, dy = (t.reshape(groups, -1, *t.shape[1:]) for t in (x, dy))

        def of_a_group(x, dy):
            _, back = jax.vjp(lambda w: stack(w, x), dict(zip(NAMES, weights, strict=True)))
            by_weights = back(dy)[0]
            gradients = [by_weights[name].astype(jnp.float32) for name in NAMES]
            gradients = clipped(gradients, sum(jnp.sum(g * g) for g in gradients), sum(g.size for g in gradients))
            new = [adamw(w.astype(jnp.float32), m, v, g) for w, m, v, g in zip(weights, m, v, gradients, strict=True)]
            return tuple(one[which] for which in range(3) for one in new)

        return tuple(t.reshape(-1, *t.shape[2:]) for t in jax.vmap(of_a_group)(x, dy))

    return step
```

profile of v0, /device:TPU:0, one launch (start us, length us, event | category | flops | bytes accessed | tf_op | source)
XLA Modules:
  0.0 2303.6 jit_solution(9985390895982435631)
XLA Ops:
  22.6 23.4 %fusion.188 = f32[2048,4096]{1,0:T(8,128)} fusion(bf16[2,1024,4096]{2,1,0:T(8,128)(2,1)} %param.12, bf16[1,2048,1024]{2,1,0:T(8,128)(2,1)S(1)} %copy-done.16, f32[2048]{0:T(1024)S(1)} %add_rsqrt_fusion), kind=kOutput, calls=%fused_computation.227 | convolution fusion | flops 17186160640 | bytes 46145536 | tf_op jit(solution)/vmap(jvp())/dot_general | solution.py:20
  46.0 38.1 %fusion.164 = (bf16[1,1,2048,4096]{3,2,1,0:T(8,128)(2,1)}, f32[2048,4096]{1,0:T(8,128)}) fusion(f32[2048,4096]{1,0:T(8,128)} %fusion.188, bf16[2,1024,4096]{2,1,0:T(8,128)(2,1)} %param.15, bf16[1,2048,1024]{2,1,0:T(8,128)(2,1)} %param.14, f32[2048]{0:T(1024)S(1)} %add_rsqrt_fusion), kind=kOutput, calls=%fused_computation.191 | convolution fusion | flops 17236492288 | bytes 96477184 | tf_op jit(solution)/vmap(jvp())/dot_general | solution.py:21
  84.0 24.0 %fusion.174 = (f32[2048]{0:T(1024)S(1)}, bf16[1,1,2048,1024]{2,3,1,0:T(8,128)(2,1)S(1)}) fusion(bf16[2,4096,1024]{2,1,0:T(8,128)(2,1)} %param.16, bf16[1,1,2048,4096]{3,2,1,0:T(8,128)(2,1)} %get-tuple-element.263, bf16[1,2048,1024]{1,2,0:T(8,128)(2,1)} %copy), kind=kOutput, calls=%fused_computation.213 | convolution fusion | flops 17190352896 | bytes 33562624 | tf_op jit(solution)/vmap(jvp())/dot_general | solution.py:9
  112.0 23.6 %fusion.177 = f32[2048,4096]{1,0:T(8,128)} fusion(bf16[2,1024,4096]{2,1,0:T(8,128)(2,1)} %param.12, bf16[1,1,2048,1024]{2,3,1,0:T(8,128)(2,1)S(1)} %fusion.175), kind=kOutput, calls=%fused_computation.216 | convolution fusion | flops 17179869184 | bytes 46137344 | tf_op jit(solution)/vmap(jvp())/dot_general | solution.py:20
  135.6 38.8 %fusion.163 = (bf16[1,1,2048,4096]{3,2,1,0:T(8,128)(2,1)}, f32[2048,4096]{1,0:T(8,128)}) fusion(f32[2048,4096]{1,0:T(8,128)} %fusion.177, bf16[2,1024,4096]{2,1,0:T(8,128)(2,1)} %param.15, bf16[1,1,2048,1024]{2,3,1,0:T(8,128)(2,1)} %copy-done), kind=kOutput, calls=%fused_computation.189 | convolution fusion | flops 17230200832 | bytes 96468992 | tf_op jit(solution)/vmap(jvp())/dot_general | solution.py:21
  181.0 44.3 %convert_multiply_fusion.2 = (bf16[1,1,2048,4096]{3,2,1,0:T(8,128)(2,1)}, bf16[1,1,2048,4096]{3,2,1,0:T(8,128)(2,1)}) fusion(f32[2048,4096]{1,0:T(8,128)} %fusion.177, f32[2048,4096]{1,0:T(8,128)} %get-tuple-element.270, bf16[2,4096,1024]{2,1,0:T(8,128)(2,1)} %param.16, bf16[1,2048,1024]{2,1,0:T(8,128)(2,1)} %param.17), kind=kOutput, calls=%fused_computation.172 | convolution fusion | flops 17314086912 | bytes 113246208 | tf_op jit(solution)/vmap(transpose(jvp()))/dot_general | solution.py:9
  225.4 23.1 %fusion.156 = bf16[2048,1024]{0,1:T(8,128)(2,1)S(1)} fusion(bf16[1,1,2048,4096]{3,2,1,0:T(8,128)(2,1)} %get-tuple-element.545, bf16[2,1024,4096]{2,1,0:T(8,128)(2,1)} %param.12), kind=kOutput, calls=%fused_computation.178 | convolution fusion | flops 17179869184 | bytes 29360128 | tf_op jit(solution)/vmap(transpose(jvp()))/dot_general | solution.py:20
  248.5 24.4 %fusion.176 = (f32[2048]{0:T(1024)S(1)}, bf16[2048,1024]{0,1:T(8,128)(2,1)}) fusion(bf16[1,1,2048,1024]{2,3,1,0:T(8,128)(2,1)S(1)} %copy-done.13, bf16[2048,1024]{0,1:T(8,128)(2,1)S(1)} %fusion.156, bf16[2,1024,4096]{2,1,0:T(8,128)(2,1)} %param.15, bf16[1,1,2048,4096]{3,2,1,0:T(8,128)(2,1)} %get-tuple-element.623), kind=kOutput, calls=%fused_computation.215 | convolution fusion | flops 17190352896 | bytes 37756928 | tf_op jit(solution)/vmap(transpose(jvp()))/dot_general | solution.py:21
  279.3 46.0 %convert_multiply_fusion = (bf16[1,1,2048,4096]{3,2,1,0:T(8,128)(2,1)}, bf16[1,1,2048,4096]{3,2,1,0:T(8,128)(2,1)}) fusion(f32[2048,4096]{1,0:T(8,128)} %fusion.188, f32[2048,4096]{1,0:T(8,128)} %get-tuple-element.264, bf16[2,4096,1024]{2,1,0:T(8,128)(2,1)} %param.16, bf16[1,1,2048,1024]{2,3,1,0:T(8,128)(2,1)S(1)} %fusion.199), kind=kOutput, calls=%fused_computation.170 | convolution fusion | flops 17314086912 | bytes 113246208 | tf_op jit(solution)/vmap(transpose(jvp()))/dot_general | solution.py:9
  325.3 216.7 %while.13 = (bf16[1,1,2048,1024]{2,3,1,0:T(8,128)(2,1)}, bf16[1,1,2048,4096]{3,2,1,0:T(8,128)(2,1)}, f32[1,64,4096]{2,1,0:T(8,128)S(1)}, f32[1,64,4096]{2,1,0:T(...) while((bf16[1,1,2048,1024]{2,3,1,0:T(8,128)(2,1)}, ...), condition=%wide.windowed_dot_general_cond_rs.1.clone, body=%wide.windowed_dot_general_body_rs.1.clone.sunk | while | flops 4298637312 | bytes 79692384 | solution.py:20
  341.3 10.7 collective-permute-done.4
  367.3 12.1 collective-permute-done.6
  397.9 10.5 collective-permute-done.4
  423.7 11.4 collective-permute-done.6
  453.7 9.1 collective-permute-done.4
  478.1 8.7 collective-permute-done.6
  543.7 230.0 %while.12 = (bf16[1,1,2048,1024]{2,3,1,0:T(8,128)(2,1)}, bf16[1,1,2048,4096]{3,2,1,0:T(8,128)(2,1)}, f32[1,64,4096]{2,1,0:T(8,128)S(1)}, f32[1,64,4096]{2,1,0:T(...) while((bf16[1,1,2048,1024]{2,3,1,0:T(8,128)(2,1)}, ...), condition=%wide.windowed_dot_general_cond_rs.clone, body=%wide.windowed_dot_general_body_rs.clone.sunk | while | flops 4298637312 | bytes 79692384 | solution.py:20
  558.8 19.1 collective-permute-done
  626.1 11.0 collective-permute-done.1
  734.1 10.6 collective-permute-done.1
  774.7 226.3 %while.15 = (bf16[1,1,2048,1024]{2,3,1,0:T(8,128)(2,1)}, bf16[1,1,2048,4096]{3,2,1,0:T(8,128)(2,1)}, f32[1,64,4096]{2,1,0:T(8,128)S(1)}, f32[1,64,4096]{2,1,0:T(...) while((bf16[1,1,2048,1024]{2,3,1,0:T(8,128)(2,1)}, ...), condition=%wide.windowed_dot_general_cond_rs.3.clone, body=%wide.windowed_dot_general_body_rs.3.clone.sunk | while | flops 4298637312 | bytes 79692384 | solution.py:21
  789.8 17.6 collective-permute-done.12
  826.2 8.9 collective-permute-done.15
  856.7 10.8 collective-permute-done.13
  976.3 8.7 collective-permute-start.15
  1005.4 22.7 copy.4
  1034.4 22.4 copy.2
  1063.3 233.6 %while.14 = (bf16[1,1,2048,1024]{2,3,1,0:T(8,128)(2,1)}, bf16[1,1,2048,4096]{3,2,1,0:T(8,128)(2,1)}, f32[1,64,4096]{2,1,0:T(8,128)S(1)}, f32[1,64,4096]{2,1,0:T(...) while((bf16[1,1,2048,1024]{2,3,1,0:T(8,128)(2,1)}, ...), condition=%wide.windowed_dot_general_cond_rs.2.clone, body=%wide.windowed_dot_general_body_rs.2.clone.sunk | while | flops 4298637312 | bytes 79692384 | solution.py:21
  1082.4 10.8 collective-permute-done.9
  1113.2 9.6 collective-permute-done.11
  1180.4 11.6 collective-permute-start.8
  1203.2 11.6 collective-permute-done.9
  1297.8 220.5 %while.17 = (bf16[1,1,2048,4096]{2,3,1,0:T(8,128)(2,1)}, bf16[1,1,2048,1024]{3,2,1,0:T(8,128)(2,1)}, f32[1,256,1024]{2,1,0:T(8,128)S(1)}, f32[1,256,1024]{2,1,0:...) while((bf16[1,1,2048,4096]{2,3,1,0:T(8,128)(2,1)}, ...), condition=%wide.windowed_dot_general_cond_rs.5.clone, body=%wide.windowed_dot_general_body_rs.5.clone.sunk | while | flops 4304928768 | bytes 83886720 | solution.py:9
  1337.2 9.8 collective-permute-done.22
  1394.4 9.8 collective-permute-done.22
  1450.2 9.8 collective-permute-done.22
  1505.0 9.8 collective-permute-done.22
  1519.3 229.7 %while.16 = (bf16[1,1,2048,4096]{2,3,1,0:T(8,128)(2,1)}, bf16[1,1,2048,1024]{3,2,1,0:T(8,128)(2,1)}, f32[1,256,1024]{2,1,0:T(8,128)S(1)}, f32[1,256,1024]{2,1,0:...) while((bf16[1,1,2048,4096]{2,3,1,0:T(8,128)(2,1)}, ...), condition=%wide.windowed_dot_general_cond_rs.4.clone, body=%wide.windowed_dot_general_body_rs.4.clone.sunk | while | flops 4304928768 | bytes 79692384 | solution.py:9
  1562.8 9.8 collective-permute-done.18
  1619.7 9.8 collective-permute-done.18
  1677.4 9.8 collective-permute-done.18
  1734.4 9.8 collective-permute-done.18
  1783.2 9.9 collective-permute-done.28
  1796.3 42.0 %all-reduce.10 = f32[1]{0:T(128)} all-reduce(f32[1]{0:T(128)} %bitcast.39), channel_id=13, replica_groups=mesh['rep'=2,'dp'=16] {'dp'}, use_global_device_ids=true, to_apply=%region_3.4.clone | all-reduce | flops 1 | bytes 8 | tf_op jit(solution)/vmap()/reduce_sum | solution.py:54
  1857.6 150.4 %all-gather.10.cloned.1.call-done = bf16[1,2,1024,4096]{3,2,1,0:T(8,128)(2,1)} async-done(((bf16[1,2,64,4096]{3,2,1,0:T(8,128)(2,1)}), bf16[1,2,1024,4096]{3,2,1,0:T(8,128)(2,1)}) %all-gather.10.cloned.1.call-update) | async-done | bytes 16777232 | tf_op jit(solution)/reshape | solution.py:58
  2008.0 127.2 %all-gather.12.cloned.1.call-done = bf16[1,2,1024,4096]{3,2,1,0:T(8,128)(2,1)} async-done(((bf16[1,2,64,4096]{3,2,1,0:T(8,128)(2,1)}), bf16[1,2,1024,4096]{3,2,1,0:T(8,128)(2,1)}) %all-gather.12.cloned.1.call-update) | async-done | bytes 16777232 | tf_op jit(solution)/reshape | solution.py:58
  2135.2 127.3 %all-gather.14.cloned.1.call-done = bf16[1,2,4096,1024]{3,2,1,0:T(8,128)(2,1)} async-done(((bf16[1,2,256,1024]{3,2,1,0:T(8,128)(2,1)}), bf16[1,2,4096,1024]{3,2,1,0:T(8,128)(2,1)}) %all-gather.14.cloned.1.call-update) | async-done | bytes 16777232 | tf_op jit(solution)/reshape | solution.py:58
  2262.5 16.8 copy.63
  (464 shorter events, 1161.9 us)
Async XLA Ops:
  7.2 2000.8 %all-gather.10.cloned.1.call-start = ((), (), s32[]{:S(2)}) async-start(), calls=%async_computation | async-start | bytes 17825792 | tf_op jit(solution)/reshape | solution.py:58
  325.4 26.6 %collective-permute-start.4 = (f32[1,64,4096]{2,1,0:T(8,128)S(1)}, f32[1,64,4096]{2,1,0:T(8,128)}, u32[]{:S(2)}, u32[]{:S(2)}) collective-permute-start(f32[1,64,4096]{2,1,0:T(8,128)S(1)} %broadcast_select_fusion.26), channel_id=9, source_target_pairs={{0,1},{1,2},{2,3},{3,4},{4,5},{5,6},{6,7},{7,8},{8,9},{9,10},{10,1... | collective-permute-start | bytes 3145736 | tf_op jit(solution)/vmap(transpose(jvp()))/dot_general | solution.py:20
  326.1 25.9 %collective-permute-start.5 = (f32[1,64,4096]{2,1,0:T(8,128)S(1)}, f32[1,64,4096]{2,1,0:T(8,128)}, u32[]{:S(2)}, u32[]{:S(2)}) collective-permute-start(f32[1,64,4096]{2,1,0:T(8,128)S(1)} %broadcast_select_fusion.27), channel_id=8, source_target_pairs={{0,15},{1,0},{2,1},{3,2},{4,3},{5,4},{6,5},{7,6},{8,7},{9,8},{10,9... | collective-permute-start | bytes 3145736 | tf_op jit(solution)/vmap(transpose(jvp()))/dot_general | solution.py:20
  353.8 25.5 %collective-permute-start.6 = (f32[1,64,4096]{2,1,0:T(8,128)S(1)}, f32[1,64,4096]{2,1,0:T(8,128)S(1)}, u32[]{:S(2)}, u32[]{:S(2)}) collective-permute-start(f32[1,64,4096]{2,1,0:T(8,128)S(1)} %get-tuple-element.465), channel_id=11, source_target_pairs={{0,1},{1,2},{2,3},{3,4},{4,5},{5,6},{6,7},{7,8},{8,9},{9,10},{10,1... | collective-permute-start | bytes 3145736 | tf_op jit(solution)/vmap(transpose(jvp()))/dot_general | solution.py:20
  355.7 23.6 %collective-permute-start.7 = (f32[1,64,4096]{2,1,0:T(8,128)S(1)}, f32[1,64,4096]{2,1,0:T(8,128)}, u32[]{:S(2)}, u32[]{:S(2)}) collective-permute-start(f32[1,64,4096]{2,1,0:T(8,128)S(1)} %get-tuple-element.466), channel_id=10, source_target_pairs={{0,15},{1,0},{2,1},{3,2},{4,3},{5,4},{6,5},{7,6},{8,7},{9,8},{10,9... | collective-permute-start | bytes 3145736 | tf_op jit(solution)/vmap(transpose(jvp()))/dot_general | solution.py:20
  383.1 25.3 %collective-permute-start.4 = (f32[1,64,4096]{2,1,0:T(8,128)S(1)}, f32[1,64,4096]{2,1,0:T(8,128)}, u32[]{:S(2)}, u32[]{:S(2)}) collective-permute-start(f32[1,64,4096]{2,1,0:T(8,128)S(1)} %broadcast_select_fusion.26), channel_id=9, source_target_pairs={{0,1},{1,2},{2,3},{3,4},{4,5},{5,6},{6,7},{7,8},{8,9},{9,10},{10,1... | collective-permute-start | bytes 3145736 | tf_op jit(solution)/vmap(transpose(jvp()))/dot_general | solution.py:20
  383.3 25.1 %collective-permute-start.5 = (f32[1,64,4096]{2,1,0:T(8,128)S(1)}, f32[1,64,4096]{2,1,0:T(8,128)}, u32[]{:S(2)}, u32[]{:S(2)}) collective-permute-start(f32[1,64,4096]{2,1,0:T(8,128)S(1)} %broadcast_select_fusion.27), channel_id=8, source_target_pairs={{0,15},{1,0},{2,1},{3,2},{4,3},{5,4},{6,5},{7,6},{8,7},{9,8},{10,9... | collective-permute-start | bytes 3145736 | tf_op jit(solution)/vmap(transpose(jvp()))/dot_general | solution.py:20
  410.2 24.9 %collective-permute-start.6 = (f32[1,64,4096]{2,1,0:T(8,128)S(1)}, f32[1,64,4096]{2,1,0:T(8,128)S(1)}, u32[]{:S(2)}, u32[]{:S(2)}) collective-permute-start(f32[1,64,4096]{2,1,0:T(8,128)S(1)} %get-tuple-element.465), channel_id=11, source_target_pairs={{0,1},{1,2},{2,3},{3,4},{4,5},{5,6},{6,7},{7,8},{8,9},{9,10},{10,1... | collective-permute-start | bytes 3145736 | tf_op jit(solution)/vmap(transpose(jvp()))/dot_general | solution.py:20
  410.3 24.8 %collective-permute-start.7 = (f32[1,64,4096]{2,1,0:T(8,128)S(1)}, f32[1,64,4096]{2,1,0:T(8,128)}, u32[]{:S(2)}, u32[]{:S(2)}) collective-permute-start(f32[1,64,4096]{2,1,0:T(8,128)S(1)} %get-tuple-element.466), channel_id=10, source_target_pairs={{0,15},{1,0},{2,1},{3,2},{4,3},{5,4},{6,5},{7,6},{8,7},{9,8},{10,9... | collective-permute-start | bytes 3145736 | tf_op jit(solution)/vmap(transpose(jvp()))/dot_general | solution.py:20
  438.9 23.9 %collective-permute-start.4 = (f32[1,64,4096]{2,1,0:T(8,128)S(1)}, f32[1,64,4096]{2,1,0:T(8,128)}, u32[]{:S(2)}, u32[]{:S(2)}) collective-permute-start(f32[1,64,4096]{2,1,0:T(8,128)S(1)} %broadcast_select_fusion.26), channel_id=9, source_target_pairs={{0,1},{1,2},{2,3},{3,4},{4,5},{5,6},{6,7},{7,8},{8,9},{9,10},{10,1... | collective-permute-start | bytes 3145736 | tf_op jit(solution)/vmap(transpose(jvp()))/dot_general | solution.py:20
  439.1 23.8 %collective-permute-start.5 = (f32[1,64,4096]{2,1,0:T(8,128)S(1)}, f32[1,64,4096]{2,1,0:T(8,128)}, u32[]{:S(2)}, u32[]{:S(2)}) collective-permute-start(f32[1,64,4096]{2,1,0:T(8,128)S(1)} %broadcast_select_fusion.27), channel_id=8, source_target_pairs={{0,15},{1,0},{2,1},{3,2},{4,3},{5,4},{6,5},{7,6},{8,7},{9,8},{10,9... | collective-permute-start | bytes 3145736 | tf_op jit(solution)/vmap(transpose(jvp()))/dot_general | solution.py:20
  542.0 1209.3 %collective-permute-start.25 = (f32[1,64,4096]{2,1,0:T(8,128)}, f32[1,64,4096]{2,1,0:T(8,128)}, u32[]{:S(2)}, u32[]{:S(2)}) collective-permute-start(f32[1,64,4096]{2,1,0:T(8,128)} %get-tuple-element.39), channel_id=12, source_target_pairs={{0,1},{1,2},{2,3},{3,4},{4,5},{5,6},{6,7},{7,8},{8,9},{9,10},{10,1... | collective-permute-start | bytes 3145736 | tf_op jit(solution)/vmap(transpose(jvp()))/dot_general | solution.py:20
  544.0 33.9 %collective-permute-start = (f32[1,64,4096]{2,1,0:T(8,128)S(1)}, f32[1,64,4096]{2,1,0:T(8,128)}, u32[]{:S(2)}, u32[]{:S(2)}) collective-permute-start(f32[1,64,4096]{2,1,0:T(8,128)S(1)} %broadcast_select_fusion.24), channel_id=3, source_target_pairs={{0,1},{1,2},{2,3},{3,4},{4,5},{5,6},{6,7},{7,8},{8,9},{9,10},{10,1... | collective-permute-start | bytes 3145736 | tf_op jit(solution)/vmap(transpose(jvp()))/dot_general | solution.py:20
  545.1 32.9 %collective-permute-start.1 = (f32[1,64,4096]{2,1,0:T(8,128)S(1)}, f32[1,64,4096]{2,1,0:T(8,128)}, u32[]{:S(2)}, u32[]{:S(2)}) collective-permute-start(f32[1,64,4096]{2,1,0:T(8,128)S(1)} %broadcast_select_fusion.25), channel_id=2, source_target_pairs={{0,15},{1,0},{2,1},{3,2},{4,3},{5,4},{6,5},{7,6},{8,7},{9,8},{10,9... | collective-permute-start | bytes 3145736 | tf_op jit(solution)/vmap(transpose(jvp()))/dot_general | solution.py:20
  579.8 25.3 %collective-permute-start.3 = (f32[1,64,4096]{2,1,0:T(8,128)S(1)}, f32[1,64,4096]{2,1,0:T(8,128)}, u32[]{:S(2)}, u32[]{:S(2)}) collective-permute-start(f32[1,64,4096]{2,1,0:T(8,128)S(1)} %get-tuple-element.457), channel_id=4, source_target_pairs={{0,15},{1,0},{2,1},{3,2},{4,3},{5,4},{6,5},{7,6},{8,7},{9,8},{10,9... | collective-permute-start | bytes 3145736 | tf_op jit(solution)/vmap(transpose(jvp()))/dot_general | solution.py:20
  639.0 24.6 %collective-permute-start.3 = (f32[1,64,4096]{2,1,0:T(8,128)S(1)}, f32[1,64,4096]{2,1,0:T(8,128)}, u32[]{:S(2)}, u32[]{:S(2)}) collective-permute-start(f32[1,64,4096]{2,1,0:T(8,128)S(1)} %get-tuple-element.457), channel_id=4, source_target_pairs={{0,15},{1,0},{2,1},{3,2},{4,3},{5,4},{6,5},{7,6},{8,7},{9,8},{10,9... | collective-permute-start | bytes 3145736 | tf_op jit(solution)/vmap(transpose(jvp()))/dot_general | solution.py:20
  746.6 24.6 %collective-permute-start.3 = (f32[1,64,4096]{2,1,0:T(8,128)S(1)}, f32[1,64,4096]{2,1,0:T(8,128)}, u32[]{:S(2)}, u32[]{:S(2)}) collective-permute-start(f32[1,64,4096]{2,1,0:T(8,128)S(1)} %get-tuple-element.457), channel_id=4, source_target_pairs={{0,15},{1,0},{2,1},{3,2},{4,3},{5,4},{6,5},{7,6},{8,7},{9,8},{10,9... | collective-permute-start | bytes 3145736 | tf_op jit(solution)/vmap(transpose(jvp()))/dot_general | solution.py:20
  773.7 986.4 %collective-permute-start.24 = (f32[1,64,4096]{2,1,0:T(8,128)}, f32[1,64,4096]{2,1,0:T(8,128)}, u32[]{:S(2)}, u32[]{:S(2)}) collective-permute-start(f32[1,64,4096]{2,1,0:T(8,128)} %get-tuple-element.37), channel_id=6, source_target_pairs={{0,1},{1,2},{2,3},{3,4},{4,5},{5,6},{6,7},{7,8},{8,9},{9,10},{10,1... | collective-permute-start | bytes 3145736 | tf_op jit(solution)/vmap(transpose(jvp()))/dot_general | solution.py:20
  774.7 32.6 %collective-permute-start.12 = (f32[1,64,4096]{2,1,0:T(8,128)S(1)}, f32[1,64,4096]{2,1,0:T(8,128)}, u32[]{:S(2)}, u32[]{:S(2)}) collective-permute-start(f32[1,64,4096]{2,1,0:T(8,128)S(1)} %broadcast_select_fusion.30), channel_id=22, source_target_pairs={{0,1},{1,2},{2,3},{3,4},{4,5},{5,6},{6,7},{7,8},{8,9},{9,10},{10,1... | collective-permute-start | bytes 3145736 | tf_op jit(solution)/vmap(transpose(jvp()))/dot_general | solution.py:21
  774.9 32.5 %collective-permute-start.13 = (f32[1,64,4096]{2,1,0:T(8,128)S(1)}, f32[1,64,4096]{2,1,0:T(8,128)}, u32[]{:S(2)}, u32[]{:S(2)}) collective-permute-start(f32[1,64,4096]{2,1,0:T(8,128)S(1)} %broadcast_select_fusion.31), channel_id=21, source_target_pairs={{0,15},{1,0},{2,1},{3,2},{4,3},{5,4},{6,5},{7,6},{8,7},{9,8},{10,9... | collective-permute-start | bytes 3145736 | tf_op jit(solution)/vmap(transpose(jvp()))/dot_general | solution.py:21
  809.7 25.4 %collective-permute-start.15 = (f32[1,64,4096]{2,1,0:T(8,128)S(1)}, f32[1,64,4096]{2,1,0:T(8,128)}, u32[]{:S(2)}, u32[]{:S(2)}) collective-permute-start(f32[1,64,4096]{2,1,0:T(8,128)S(1)} %get-tuple-element.484), channel_id=23, source_target_pairs={{0,15},{1,0},{2,1},{3,2},{4,3},{5,4},{6,5},{7,6},{8,7},{9,8},{10,9... | collective-permute-start | bytes 3145736 | tf_op jit(solution)/vmap(transpose(jvp()))/dot_general | solution.py:21
  869.4 24.6 %collective-permute-start.15 = (f32[1,64,4096]{2,1,0:T(8,128)S(1)}, f32[1,64,4096]{2,1,0:T(8,128)}, u32[]{:S(2)}, u32[]{:S(2)}) collective-permute-start(f32[1,64,4096]{2,1,0:T(8,128)S(1)} %get-tuple-element.484), channel_id=23, source_target_pairs={{0,15},{1,0},{2,1},{3,2},{4,3},{5,4},{6,5},{7,6},{8,7},{9,8},{10,9... | collective-permute-start | bytes 3145736 | tf_op jit(solution)/vmap(transpose(jvp()))/dot_general | solution.py:21
  946.6 23.0 collective-permute-start.12
  1001.9 760.1 %collective-permute-start.27 = (f32[1,64,4096]{2,1,0:T(8,128)}, f32[1,64,4096]{2,1,0:T(8,128)}, u32[]{:S(2)}, u32[]{:S(2)}) collective-permute-start(f32[1,64,4096]{2,1,0:T(8,128)} %get-tuple-element.43), channel_id=25, source_target_pairs={{0,1},{1,2},{2,3},{3,4},{4,5},{5,6},{6,7},{7,8},{8,9},{9,10},{10,1... | collective-permute-start | bytes 3145736 | tf_op jit(solution)/vmap(transpose(jvp()))/dot_general | solution.py:21
  1065.4 27.8 %collective-permute-start.9 = (f32[1,64,4096]{2,1,0:T(8,128)}, f32[1,64,4096]{2,1,0:T(8,128)}, u32[]{:S(2)}, u32[]{:S(2)}) collective-permute-start(f32[1,64,4096]{2,1,0:T(8,128)} %broadcast_select_fusion.29), channel_id=15, source_target_pairs={{0,15},{1,0},{2,1},{3,2},{4,3},{5,4},{6,5},{7,6},{8,7},{9,8},{10,9... | collective-permute-start | bytes 3145736 | tf_op jit(solution)/vmap(transpose(jvp()))/dot_general | solution.py:21
  1099.8 23.1 %collective-permute-start.11 = (f32[1,64,4096]{2,1,0:T(8,128)S(1)}, f32[1,64,4096]{2,1,0:T(8,128)}, u32[]{:S(2)}, u32[]{:S(2)}) collective-permute-start(f32[1,64,4096]{2,1,0:T(8,128)S(1)} %get-tuple-element.475), channel_id=17, source_target_pairs={{0,15},{1,0},{2,1},{3,2},{4,3},{5,4},{6,5},{7,6},{8,7},{9,8},{10,9... | collective-permute-start | bytes 3145736 | tf_op jit(solution)/vmap(transpose(jvp()))/dot_general | solution.py:21
  1129.1 23.0 collective-permute-start.9
  1217.6 23.7 %collective-permute-start.11 = (f32[1,64,4096]{2,1,0:T(8,128)S(1)}, f32[1,64,4096]{2,1,0:T(8,128)}, u32[]{:S(2)}, u32[]{:S(2)}) collective-permute-start(f32[1,64,4096]{2,1,0:T(8,128)S(1)} %get-tuple-element.475), channel_id=17, source_target_pairs={{0,15},{1,0},{2,1},{3,2},{4,3},{5,4},{6,5},{7,6},{8,7},{9,8},{10,9... | collective-permute-start | bytes 3145736 | tf_op jit(solution)/vmap(transpose(jvp()))/dot_general | solution.py:21
  1271.2 22.9 collective-permute-start.11
  1352.3 23.0 collective-permute-start.20
  1379.9 24.3 %collective-permute-start.22 = (f32[1,256,1024]{2,1,0:T(8,128)}, f32[1,256,1024]{2,1,0:T(8,128)S(1)}, u32[]{:S(2)}, u32[]{:S(2)}) collective-permute-start(f32[1,256,1024]{2,1,0:T(8,128)} %get-tuple-element.501), channel_id=37, source_target_pairs={{0,1},{1,2},{2,3},{3,4},{4,5},{5,6},{6,7},{7,8},{8,9},{9,10},{10,1... | collective-permute-start | bytes 3145736 | tf_op jit(solution)/vmap(transpose(jvp()))/dot_general | solution.py:9
  1380.0 25.3 %collective-permute-start.23 = (f32[1,256,1024]{2,1,0:T(8,128)S(1)}, f32[1,256,1024]{2,1,0:T(8,128)}, u32[]{:S(2)}, u32[]{:S(2)}) collective-permute-start(f32[1,256,1024]{2,1,0:T(8,128)S(1)} %get-tuple-element.502), channel_id=36, source_target_pairs={{0,15},{1,0},{2,1},{3,2},{4,3},{5,4},{6,5},{7,6},{8,7},{9,8},{10,9... | collective-permute-start | bytes 3145736 | tf_op jit(solution)/vmap(transpose(jvp()))/dot_general | solution.py:9
  1434.4 25.6 %collective-permute-start.22 = (f32[1,256,1024]{2,1,0:T(8,128)}, f32[1,256,1024]{2,1,0:T(8,128)S(1)}, u32[]{:S(2)}, u32[]{:S(2)}) collective-permute-start(f32[1,256,1024]{2,1,0:T(8,128)} %get-tuple-element.501), channel_id=37, source_target_pairs={{0,1},{1,2},{2,3},{3,4},{4,5},{5,6},{6,7},{7,8},{8,9},{9,10},{10,1... | collective-permute-start | bytes 3145736 | tf_op jit(solution)/vmap(transpose(jvp()))/dot_general | solution.py:9
  1436.9 24.1 %collective-permute-start.23 = (f32[1,256,1024]{2,1,0:T(8,128)S(1)}, f32[1,256,1024]{2,1,0:T(8,128)}, u32[]{:S(2)}, u32[]{:S(2)}) collective-permute-start(f32[1,256,1024]{2,1,0:T(8,128)S(1)} %get-tuple-element.502), channel_id=36, source_target_pairs={{0,15},{1,0},{2,1},{3,2},{4,3},{5,4},{6,5},{7,6},{8,7},{9,8},{10,9... | collective-permute-start | bytes 3145736 | tf_op jit(solution)/vmap(transpose(jvp()))/dot_general | solution.py:9
  1489.5 25.3 %collective-permute-start.22 = (f32[1,256,1024]{2,1,0:T(8,128)}, f32[1,256,1024]{2,1,0:T(8,128)S(1)}, u32[]{:S(2)}, u32[]{:S(2)}) collective-permute-start(f32[1,256,1024]{2,1,0:T(8,128)} %get-tuple-element.501), channel_id=37, source_target_pairs={{0,1},{1,2},{2,3},{3,4},{4,5},{5,6},{6,7},{7,8},{8,9},{9,10},{10,1... | collective-permute-start | bytes 3145736 | tf_op jit(solution)/vmap(transpose(jvp()))/dot_general | solution.py:9
  1493.5 22.9 collective-permute-start.23
  1546.7 25.9 %collective-permute-start.18 = (f32[1,256,1024]{2,1,0:T(8,128)}, f32[1,256,1024]{2,1,0:T(8,128)}, u32[]{:S(2)}, u32[]{:S(2)}) collective-permute-start(f32[1,256,1024]{2,1,0:T(8,128)} %get-tuple-element.492), channel_id=31, source_target_pairs={{0,1},{1,2},{2,3},{3,4},{4,5},{5,6},{6,7},{7,8},{8,9},{9,10},{10,1... | collective-permute-start | bytes 3145736 | tf_op jit(solution)/vmap(transpose(jvp()))/dot_general | solution.py:9
  1550.8 22.9 collective-permute-start.19
  1605.2 24.4 %collective-permute-start.18 = (f32[1,256,1024]{2,1,0:T(8,128)}, f32[1,256,1024]{2,1,0:T(8,128)}, u32[]{:S(2)}, u32[]{:S(2)}) collective-permute-start(f32[1,256,1024]{2,1,0:T(8,128)} %get-tuple-element.492), channel_id=31, source_target_pairs={{0,1},{1,2},{2,3},{3,4},{4,5},{5,6},{6,7},{7,8},{8,9},{9,10},{10,1... | collective-permute-start | bytes 3145736 | tf_op jit(solution)/vmap(transpose(jvp()))/dot_general | solution.py:9
  1608.4 22.9 collective-permute-start.19
  1663.1 24.1 %collective-permute-start.18 = (f32[1,256,1024]{2,1,0:T(8,128)}, f32[1,256,1024]{2,1,0:T(8,128)}, u32[]{:S(2)}, u32[]{:S(2)}) collective-permute-start(f32[1,256,1024]{2,1,0:T(8,128)} %get-tuple-element.492), channel_id=31, source_target_pairs={{0,1},{1,2},{2,3},{3,4},{4,5},{5,6},{6,7},{7,8},{8,9},{9,10},{10,1... | collective-permute-start | bytes 3145736 | tf_op jit(solution)/vmap(transpose(jvp()))/dot_general | solution.py:9
  1665.0 22.9 collective-permute-start.19
  1719.4 24.8 %collective-permute-start.18 = (f32[1,256,1024]{2,1,0:T(8,128)}, f32[1,256,1024]{2,1,0:T(8,128)}, u32[]{:S(2)}, u32[]{:S(2)}) collective-permute-start(f32[1,256,1024]{2,1,0:T(8,128)} %get-tuple-element.492), channel_id=31, source_target_pairs={{0,1},{1,2},{2,3},{3,4},{4,5},{5,6},{6,7},{7,8},{8,9},{9,10},{10,1... | collective-permute-start | bytes 3145736 | tf_op jit(solution)/vmap(transpose(jvp()))/dot_general | solution.py:9
  1723.2 22.9 collective-permute-start.19
  1751.2 30.6 %collective-permute-start.29 = (f32[1,256,1024]{2,1,0:T(8,128)}, f32[1,256,1024]{2,1,0:T(8,128)}, u32[]{:S(2)}, u32[]{:S(2)}) collective-permute-start(f32[1,256,1024]{2,1,0:T(8,128)} %copy-done.10), channel_id=38, source_target_pairs={{0,1},{1,2},{2,3},{3,4},{4,5},{5,6},{6,7},{7,8},{8,9},{9,10},{10,1... | collective-permute-start | bytes 3145736 | tf_op jit(solution)/vmap(transpose(jvp()))/dot_general | solution.py:9
  1751.3 41.8 %collective-permute-start.28 = (f32[1,256,1024]{2,1,0:T(8,128)}, f32[1,256,1024]{2,1,0:T(8,128)}, u32[]{:S(2)}, u32[]{:S(2)}) collective-permute-start(f32[1,256,1024]{2,1,0:T(8,128)} %get-tuple-element.45), channel_id=32, source_target_pairs={{0,1},{1,2},{2,3},{3,4},{4,5},{5,6},{6,7},{7,8},{8,9},{9,10},{10,1... | collective-permute-start | bytes 3145736 | tf_op jit(solution)/vmap(transpose(jvp()))/dot_general | solution.py:9
  1845.3 290.0 %all-gather.12.cloned.1.call-start = ((), (), s32[]{:S(2)}) async-start(), calls=%async_computation.1 | async-start | bytes 17825792 | tf_op jit(solution)/reshape | solution.py:58
  1851.4 411.1 %all-gather.14.cloned.1.call-start = ((), (), s32[]{:S(2)}) async-start(), calls=%async_computation.2 | async-start | bytes 17825792 | tf_op jit(solution)/reshape | solution.py:58
  (93 other events, 2068.4 us)
Sparse Core Ops, SparseCore 0:
  1845.4 162.5 all-gather.9
  2010.8 124.3 all-gather.11
  2138.1 124.3 all-gather.13
where the time goes:
time: 2320 us; the launch traced here: 2300 us
  waiting for transfers between devices  921 us (40%)
  matrix products  634 us (27%)
  starting transfers between devices  304 us (13%)
  other arithmetic  205 us (9%)
  local copies, waits for them, and re-layouts  131 us (6%)
  loops' own time  48 us (2%)
  blocking collectives  42 us (2%)
    reshape x3, waiting for transfers between devices, step(): t.reshape(-1, *t.shape[2:])  405 us
    dot_general x19, matrix products, layer(): up = jnp.dot(a, w['w_up'], preferred_element_type=jnp.float32)  234 us
    dot_general x19, matrix products, layer(): gate = jnp.dot(a, w['w_gate'], preferred_element_type=jnp.float32)  203 us
    dot_general x19, matrix products, matmul(): jnp.dot(a, w, preferred_element_type=jnp.float32).astype(jnp.bfloat16)  197 us
    dot_general x34, waiting for transfers between devices, matmul(): jnp.dot(a, w, preferred_element_type=jnp.float32).astype(jnp.bfloat16)  183 us
    dot_general x34, waiting for transfers between devices, layer(): gate = jnp.dot(a, w['w_gate'], preferred_element_type=jnp.float32)  174 us
    dot_general x34, waiting for transfers between devices, layer(): up = jnp.dot(a, w['w_up'], preferred_element_type=jnp.float32)  159 us
    dot_general x34, starting transfers between devices, matmul(): jnp.dot(a, w, preferred_element_type=jnp.float32).astype(jnp.bfloat16)  125 us
  transfers between devices with their start and end apart: 105, of which 90 were waited for; matrix products, arithmetic and copies ran while one was open for 25% of the time, Pallas kernels for 0%

commit v1 on v0

v1 whole, which is shorter than its diff:
```python
import jax
import jax.numpy as jnp
from jax import lax
from jax.sharding import PartitionSpec as P

NAMES = ("w_gate", "w_up", "w_down")
F32, BF16 = jnp.float32, jnp.bfloat16


def dot(a, b, ca, cb):
    return lax.dot_general(a, b, (((ca,), (cb,)), ((), ())), preferred_element_type=F32)


def normed(h):
    wide = h.astype(F32)
    scale = lax.rsqrt(jnp.mean(wide**2, -1, keepdims=True) + 1e-6)
    return (wide * scale).astype(BF16)


def act(gate, up):
    return (jax.nn.silu(gate) * up).astype(BF16)


def act_back(gate, up, dhid):
    d = dhid.astype(F32)
    s = jax.nn.sigmoid(gate)
    silu = gate * s
    return (d * up * (s * (1 + gate * (1 - s)))).astype(BF16), (d * silu).astype(BF16)


def adamw(w, m, v, g):
    m = 0.9 * m + 0.1 * g
    v = 0.95 * v + 0.05 * g * g
    step = m * lax.rsqrt(v + 1e-8) + 0.1 * w
    return (w - 0.02 * step).astype(BF16), m, v


def solution(mesh):
    n = mesh.shape["dp"]

    def body(x, dy, wg, wu, wd, *mv):
        h0, dy = x[0], dy[0]
        m, v = mv[:3], mv[3:]

        def scatter(g):
            return lax.psum_scatter(g, "dp", scatter_dimension=0, tiled=True)

        a0 = normed(h0)
        g0, u0 = dot(a0, wg[0], 1, 0), dot(a0, wu[0], 1, 0)
        hid0 = act(g0, u0)
        h1 = h0 + dot(hid0, wd[0], 1, 0).astype(BF16)
        a1, norm_back = jax.vjp(normed, h1)
        g1, u1 = dot(a1, wg[1], 1, 0), dot(a1, wu[1], 1, 0)
        hid1 = act(g1, u1)
        d_down1 = scatter(dot(hid1, dy, 0, 0).astype(BF16))
        dhid1 = dot(dy, wd[1], 1, 1).astype(BF16)
        dg1, du1 = act_back(g1, u1, dhid1)
        d_gate1 = scatter(dot(a1, dg1, 0, 0).astype(BF16))
        d_up1 = scatter(dot(a1, du1, 0, 0).astype(BF16))
        da1 = dot(dg1, wg[1], 1, 1).astype(BF16) + dot(du1, wu[1], 1, 1).astype(BF16)
        dh1 = dy + norm_back(da1)[0]
        d_down0 = scatter(dot(hid0, dh1, 0, 0).astype(BF16))
        dhid0 = dot(dh1, wd[0], 1, 1).astype(BF16)
        dg0, du0 = act_back(g0, u0, dhid0)
        d_gate0 = scatter(dot(a0, dg0, 0, 0).astype(BF16))
        d_up0 = scatter(dot(a0, du0, 0, 0).astype(BF16))
        gs = [(d_gate0, d_gate1), (d_up0, d_up1), (d_down0, d_down1)]
        total = sum(jnp.sum(jnp.square(g.astype(F32))) for pair in gs for g in pair)
        total = lax.psum(total, "dp")
        count = sum(w.size for w in (wg, wu, wd))
        factor = jnp.minimum(1.0, 0.5 * lax.rsqrt(total / count + 1e-30))
        me = lax.axis_index("dp")
        news, ms, vs = [], [], []
        for w, mm, vv, pair in zip((wg, wu, wd), m, v, gs):
            rows = w.shape[1] // n
            own = lax.dynamic_slice_in_dim(w, me * rows, rows, 1)
            g = jnp.stack([p.astype(F32) for p in pair]) * factor
            new, nm, nv = adamw(own.astype(F32), mm, vv, g)
            news.append(lax.all_gather(new, "dp", axis=1, tiled=True))
            ms.append(nm)
            vs.append(nv)
        return (*news, *ms, *vs)

    seq, whole, shard = P(("rep", "dp")), P(), P(None, "dp")
    return jax.shard_map(
        body,
        mesh=mesh,
        in_specs=(seq, seq, whole, whole, whole, *([shard] * 6)),
        out_specs=(*([P("rep")] * 3), *([P("rep", "dp")] * 6)),
        check_vma=False,
    )
```

time: 2320 us -> 1340 us (0.58)
  starting transfers between devices: 304 us -> 0.37 us
  matrix products: 634 us -> 416 us
  other arithmetic: 205 us -> 38.7 us
  waiting for transfers between devices: 921 us -> 782 us
  local copies, waits for them, and re-layouts: 131 us -> 47.7 us
  loops' own time: 48 us -> 0 us
    dot_general x102 -> x0, waiting for transfers between devices: 516 us -> none  [the longest x34 183 us: matmul(): jnp.dot(a, w, preferred_element_type=jnp.float32).astype(jnp.bfloat16)]
    reduce_scatter x0 -> x6, waiting for transfers between devices: none -> 416 us  [scatter(): return lax.psum_scatter(g, 'dp', scatter_dimension=0, tiled=True)]
    reshape x3 -> x0, waiting for transfers between devices: 405 us -> none  [step(): t.reshape(-1, *t.shape[2:])]
    all_gather x0 -> x3, waiting for transfers between devices: none -> 366 us  [body(): news.append(lax.all_gather(new, 'dp', axis=1, tiled=True))]
    dot_general x102 -> x0, starting transfers between devices: 304 us -> none  [the longest x34 125 us: matmul(): jnp.dot(a, w, preferred_element_type=jnp.float32).astype(jnp.bfloat16)]
    dot_general x57 -> x15, matrix products: 634 us -> 416 us  [dot(): lax.dot_general(a, b, (((ca,), (cb,)), ((), ())), preferred_element_type=...]
    dot_general x96 -> x0, other arithmetic: 159 us -> none  [the longest x16 42.9 us: matmul(): jnp.dot(a, w, preferred_element_type=jnp.float32).astype(jnp.bfloat16)]
    unnamed x73 -> x43, local copies, waits for them, and re-layouts: 112 us -> 47.7 us
  transfers between devices with their start and end apart: 105 -> 9, of which waited for: 90 -> 7; matrix products, arithmetic and copies ran while one was open for 25% -> 18% of each run, Pallas kernels for 0% -> 0%
where the time goes in v1:
time: 1340 us
  waiting for transfers between devices  782 us (58%)
  matrix products  416 us (31%)
  local copies, waits for them, and re-layouts  47.7 us (4%)
  other arithmetic  38.7 us (3%)
  blocking collectives  32.2 us (2%)
  between operations  19.1 us (1%)
    reduce_scatter x6, waiting for transfers between devices, scatter(): return lax.psum_scatter(g, 'dp', scatter_dimension=0, tiled=True)  416 us
    dot_general x15, matrix products, dot(): lax.dot_general(a, b, (((ca,), (cb,)), ((), ())), preferred_element_type=...  416 us
    all_gather x3, waiting for transfers between devices, body(): news.append(lax.all_gather(new, 'dp', axis=1, tiled=True))  366 us
    unnamed x43, local copies, waits for them, and re-layouts  47.7 us
    psum x1, blocking collectives, body(): total = lax.psum(total, 'dp')  32.2 us
  transfers between devices with their start and end apart: 9, of which 7 were waited for; matrix products, arithmetic and copies ran while one was open for 18% of the time, Pallas kernels for 0%

profile of v1, /device:TPU:0, one launch (start us, length us, event | category | flops | bytes accessed | tf_op | source)
XLA Modules:
  0.0 1335.8 jit_solution(12784956640642316721)
XLA Ops:
  7.2 6.6 copy.20
  13.8 3.1 fusion.13
  16.9 24.4 %fusion.33 = f32[2048,4096]{1,0:T(8,128)} fusion(bf16[2,1024,4096]{2,1,0:T(8,128)(2,1)} %param.13, bf16[1,2048,1024]{2,1,0:T(8,128)(2,1)} %param.11, f32[2048]{0:T(1024)S(1)} %add_rsqrt_fusion), kind=kOutput, calls=%fused_computation.48 | convolution fusion | flops 17186160640 | bytes 46145536 | tf_op jit(solution)/shard_map/dot_general | solution.py:11
  41.2 38.1 %multiply_convert_fusion.1 = (bf16[2048,4096]{1,0:T(8,128)(2,1)}, f32[2048,4096]{1,0:T(8,128)}) fusion(f32[2048,4096]{1,0:T(8,128)} %fusion.33, bf16[2,1024,4096]{2,1,0:T(8,128)(2,1)} %param.14, bf16[1,2048,1024]{2,1,0:T(8,128)(2,1)} %param.11, f32[2048]{0:T(1024)S(1)} %add_rsqrt_fusion), kind=kOutput, calls=%fused_computation.13 | convolution fusion | flops 17236492288 | bytes 96477184 | tf_op jit(solution)/shard_map/dot_general | solution.py:11
  79.3 24.0 %fusion.17 = (f32[2048]{0:T(1024)S(1)}, bf16[2048,1024]{0,1:T(8,128)(2,1)S(1)}) fusion(bf16[2048,4096]{1,0:T(8,128)(2,1)} %get-tuple-element.20, bf16[2,4096,1024]{2,1,0:T(8,128)(2,1)} %param.15, bf16[1,2048,1024]{1,2,0:T(8,128)(2,1)} %copy.20), kind=kOutput, calls=%fused_computation.32 | convolution fusion | flops 17190352896 | bytes 33562624 | tf_op jit(solution)/shard_map/dot_general | solution.py:11
  103.4 24.7 %fusion.26 = f32[2048,4096]{1,0:T(8,128)} fusion(bf16[2,1024,4096]{2,1,0:T(8,128)(2,1)} %param.14, bf16[2048,1024]{0,1:T(8,128)(2,1)S(1)} %get-tuple-element.23, f32[2048]{0:T(1024)S(1)} %fusion.88), kind=kOutput, calls=%fused_computation.41 | convolution fusion | flops 17186160640 | bytes 46145536 | tf_op jit(solution)/shard_map/dot_general | solution.py:11
  128.1 23.4 %fusion.22 = f32[2048,4096]{1,0:T(8,128)} fusion(bf16[2,1024,4096]{2,1,0:T(8,128)(2,1)} %param.13, bf16[2048,1024]{0,1:T(8,128)(2,1)S(1)} %get-tuple-element.23, f32[2048]{0:T(1024)S(1)} %fusion.88), kind=kOutput, calls=%fused_computation.37 | convolution fusion | flops 17186160640 | bytes 46145536 | tf_op jit(solution)/shard_map/dot_general | solution.py:11
  151.5 44.3 %fusion.2 = (bf16[2048,4096]{1,0:T(8,128)(2,1)}, bf16[2048,4096]{1,0:T(8,128)(2,1)}) fusion(f32[2048,4096]{1,0:T(8,128)} %fusion.22, f32[2048,4096]{1,0:T(8,128)} %fusion.26, bf16[2,4096,1024]{2,1,0:T(8,128)(2,1)} %param.15, bf16[1,2048,1024]{2,1,0:T(8,128)(2,1)} %param.12), kind=kOutput, calls=%fused_computation.6 | convolution fusion | flops 17305698304 | bytes 113246208 | tf_op jit(solution)/shard_map/dot_general | solution.py:11
  195.7 22.9 %convolution_convert_fusion.4 = bf16[1024,4096]{1,0:T(8,128)(2,1)} fusion(bf16[2048,4096]{1,0:T(8,128)(2,1)} %get-tuple-element.19, bf16[2048,1024]{0,1:T(8,128)(2,1)} %copy-done.2, f32[2048]{0:T(1024)S(1)} %fusion.88), kind=kOutput, calls=%fused_computation.60 | convolution fusion | flops 17190354944 | bytes 29368320 | tf_op jit(solution)/shard_map/dot_general | solution.py:11
  218.7 24.0 %fusion.20 = bf16[2048,1024]{0,1:T(8,128)(2,1)} fusion(bf16[2048,4096]{1,0:T(8,128)(2,1)} %get-tuple-element.19, bf16[2,1024,4096]{2,1,0:T(8,128)(2,1)} %param.13), kind=kOutput, calls=%fused_computation.35 | convolution fusion | flops 17179869184 | bytes 29360128 | tf_op jit(solution)/shard_map/dot_general | solution.py:11
  242.7 6.4 copy.21
  249.2 24.5 %fusion.19 = (f32[2048]{0:T(1024)S(1)}, bf16[2048,1024]{0,1:T(8,128)(2,1)S(1)}) fusion(bf16[2048,1024]{0,1:T(8,128)(2,1)} %copy-done.2, bf16[2048,1024]{0,1:T(8,128)(2,1)} %fusion.20, bf16[2048,4096]{1,0:T(8,128)(2,1)} %get-tuple-element.18, bf16[2,1024,4096]{2,1,0:T(8,128)(2,1)} %param.14), kind=kOutput, calls=%fused_computation.34 | convolution fusion | flops 17192450048 | bytes 37756928 | tf_op jit(solution)/shard_map/dot_general | solution.py:11
  273.7 4.8 fusion.55
  278.5 25.2 %convolution_convert_fusion = bf16[2048,4096]{1,0:T(8,128)(2,1)} fusion(bf16[2048,1024]{0,1:T(8,128)(2,1)} %fusion.55, bf16[2,4096,1024]{2,1,0:T(8,128)(2,1)} %param.15), kind=kOutput, calls=%fused_computation.19 | convolution fusion | flops 17188257792 | bytes 29360128 | tf_op jit(solution)/shard_map/dot_general | solution.py:11
  303.7 35.8 %fusion.39 = bf16[1024,4096]{1,0:T(8,128)(2,1)} fusion(f32[2048,4096]{1,0:T(8,128)} %get-tuple-element.21, bf16[2048,4096]{1,0:T(8,128)(2,1)} %convolution_convert_fusion, f32[2048,4096]{1,0:T(8,128)} %fusion.33, bf16[1,2048,1024]{1,2,0:T(8,128)(2,1)} %copy.20, f32[2048]{0:T(1024)S(1)} %copy-done.14), kind=kOutput, calls=%fused_computation.55 | convolution fusion | flops 17282629632 | bytes 96477184 | tf_op jit(solution)/shard_map/dot_general | solution.py:11
  339.6 26.8 %fusion.42 = bf16[1024,4096]{1,0:T(8,128)(2,1)} fusion(bf16[2048,4096]{1,0:T(8,128)(2,1)} %convolution_convert_fusion, f32[2048,4096]{1,0:T(8,128)} %fusion.33, bf16[1,2048,1024]{1,2,0:T(8,128)(2,1)} %copy.20, f32[2048]{0:T(1024)S(1)} %copy-done.14), kind=kOutput, calls=%fused_computation.56 | convolution fusion | flops 17249075200 | bytes 62922752 | tf_op jit(solution)/shard_map/dot_general | solution.py:11
  366.4 0.6 copy-done.10
  367.1 23.0 %convolution_convert_fusion.3 = bf16[1024,4096]{1,0:T(8,128)(2,1)} fusion(bf16[2048,4096]{1,0:T(8,128)(2,1)} %get-tuple-element.18, bf16[2048,1024]{0,1:T(8,128)(2,1)} %copy-done.2, f32[2048]{0:T(1024)S(1)} %copy-done.10), kind=kOutput, calls=%fused_computation.59 | convolution fusion | flops 17190354944 | bytes 29368320 | tf_op jit(solution)/shard_map/dot_general | solution.py:11
  390.2 24.1 %convolution_convert_fusion.2 = bf16[4096,1024]{1,0:T(8,128)(2,1)} fusion(bf16[2048,4096]{1,0:T(8,128)(2,1)} %get-tuple-element.20, bf16[2048,1024]{0,1:T(8,128)(2,1)} %fusion.55), kind=kOutput, calls=%fused_computation.58 | convolution fusion | flops 17184063488 | bytes 29360128 | tf_op jit(solution)/shard_map/dot_general | solution.py:11
  414.3 30.8 %fusion.45 = bf16[4096,1024]{1,0:T(8,128)(2,1)} fusion(f32[2048,4096]{1,0:T(8,128)} %fusion.26, f32[2048,4096]{1,0:T(8,128)} %fusion.22, bf16[1,2048,1024]{2,1,0:T(8,128)(2,1)} %param.12), kind=kOutput, calls=%fused_computation.57 | convolution fusion | flops 17234395136 | bytes 79691776 | tf_op jit(solution)/shard_map/dot_general | solution.py:11
  445.2 2.0 fusion.83
  447.2 1.9 fusion.82
  450.4 102.2 %reduce-scatter.11.cloned.1.call-done = bf16[64,4096]{1,0:T(8,128)(2,1)} async-done(((bf16[1024,4096]{1,0:T(8,128)(2,1)}), bf16[64,4096]{1,0:T(8,128)(2,1)}) %reduce-scatter.11.cloned.1.call-update) | async-done | bytes 524304 | tf_op jit(solution)/shard_map/reduce_scatter | solution.py:46
  552.6 1.9 fusion.84
  555.2 104.7 %reduce-scatter.13.cloned.1.call-done = bf16[64,4096]{1,0:T(8,128)(2,1)} async-done(((bf16[1024,4096]{1,0:T(8,128)(2,1)}), bf16[64,4096]{1,0:T(8,128)(2,1)}) %reduce-scatter.13.cloned.1.call-update) | async-done | bytes 524304 | tf_op jit(solution)/shard_map/reduce_scatter | solution.py:46
  659.8 1.9 fusion.85
  662.4 104.7 %reduce-scatter.15.cloned.1.call-done = bf16[256,1024]{1,0:T(8,128)(2,1)} async-done(((bf16[4096,1024]{1,0:T(8,128)(2,1)}), bf16[256,1024]{1,0:T(8,128)(2,1)}) %reduce-scatter.15.cloned.1.call-update) | async-done | bytes 524304 | tf_op jit(solution)/shard_map/reduce_scatter | solution.py:46
  767.1 1.9 fusion.86
  769.6 104.7 %reduce-scatter.17.cloned.1.call-done = bf16[256,1024]{1,0:T(8,128)(2,1)} async-done(((bf16[4096,1024]{1,0:T(8,128)(2,1)}), bf16[256,1024]{1,0:T(8,128)(2,1)}) %reduce-scatter.17.cloned.1.call-update) | async-done | bytes 524304 | tf_op jit(solution)/shard_map/reduce_scatter | solution.py:46
  874.3 1.9 fusion.87
  876.9 32.2 %psum.7 = f32[]{:T(128)} all-reduce(f32[]{:T(128)S(6)} %add.134), channel_id=1, replica_groups=mesh['rep'=2,'dp'=16] {'dp'}, use_global_device_ids=true, to_apply=%region_15.16 | all-reduce | flops 1 | bytes 8 | tf_op jit(solution)/shard_map/psum | solution.py:69
  909.7 1.2 convert_bitcast_fusion.1
  910.9 1.1 convert_bitcast_fusion
  912.1 5.0 fusion.76
  917.2 0.1 convert_bitcast_fusion.2
  917.3 1.2 convert_bitcast_fusion.3
  918.5 5.6 fusion.73
  924.2 0.1 convert_bitcast_fusion.4
  924.3 0.1 convert_bitcast_fusion.5
  924.4 4.8 fusion.70
  929.2 111.0 %all-gather.8.cloned.1.call-done = bf16[2,4096,1024]{2,1,0:T(8,128)(2,1)} async-done(((bf16[2,256,1024]{2,1,0:T(8,128)(2,1)}), bf16[2,4096,1024]{2,1,0:T(8,128)(2,1)}) %all-gather.8.cloned.1.call-update) | async-done | bytes 16777232 | tf_op jit(solution)/shard_map/all_gather | solution.py:79
  1040.2 127.2 %all-gather.6.cloned.1.call-done = bf16[2,1024,4096]{2,1,0:T(8,128)(2,1)} async-done(((bf16[2,64,4096]{2,1,0:T(8,128)(2,1)}), bf16[2,1024,4096]{2,1,0:T(8,128)(2,1)}) %all-gather.6.cloned.1.call-update) | async-done | bytes 16777232 | tf_op jit(solution)/shard_map/all_gather | solution.py:79
  1167.5 127.3 %all-gather.4.cloned.1.call-done = bf16[2,1024,4096]{2,1,0:T(8,128)(2,1)} async-done(((bf16[2,64,4096]{2,1,0:T(8,128)(2,1)}), bf16[2,1024,4096]{2,1,0:T(8,128)(2,1)}) %all-gather.4.cloned.1.call-update) | async-done | bytes 16777232 | tf_op jit(solution)/shard_map/all_gather | solution.py:79
  1294.7 16.8 %copy.25 = bf16[2,1024,4096]{2,1,0:T(8,128)(2,1)} copy(bf16[2,1024,4096]{2,1,0:T(8,128)(2,1)} %all-gather.4.cloned.1.call-done) | data formatting | bytes 33554432
  1311.5 8.5 copy.26
  1320.0 1.4 slice-done.2
  1321.5 1.2 slice-done.3
  1322.7 6.2 copy.27
  (59 shorter events, 0.6 us)
Async XLA Ops:
  7.2 438.0 %reduce-scatter.9.cloned.1.call-start = ((), (), s32[]{:S(2)}) async-start(), calls=%async_computation.7 | async-start | bytes 8912896 | tf_op jit(solution)/shard_map/reduce_scatter | solution.py:46
  16.9 24.4 %copy-start.13 = (f32[2048]{0:T(1024)}, f32[2048]{0:T(1024)S(1)}, u32[]{:S(2)}) copy-start(f32[2048]{0:T(1024)S(1)} %add_rsqrt_fusion) | copy-start | bytes 24580
  103.3 24.7 %copy-start.2 = (bf16[2048,1024]{0,1:T(8,128)(2,1)}, bf16[2048,1024]{0,1:T(8,128)(2,1)S(1)}, u32[]{:S(2)}) copy-start(bf16[2048,1024]{0,1:T(8,128)(2,1)S(1)} %get-tuple-element.23) | copy-start | bytes 12582916
  103.3 24.7 %copy-start.11 = (f32[2048]{0:T(1024)}, f32[2048]{0:T(1024)S(1)}, u32[]{:S(2)}) copy-start(f32[2048]{0:T(1024)S(1)} %get-tuple-element.22) | copy-start | bytes 24580
  103.4 170.4 %copy-start.9 = (f32[2048]{0:T(1024)}, f32[2048]{0:T(1024)S(1)}, u32[]{:S(2)}) copy-start(f32[2048]{0:T(1024)S(1)} %fusion.88) | copy-start | bytes 24580
  218.7 228.6 %reduce-scatter.7.cloned.1.call-start = ((), (), s32[]{:S(2)}) async-start(), calls=%async_computation.6 | async-start | bytes 8912896 | tf_op jit(solution)/shard_map/reduce_scatter | solution.py:46
  249.2 24.5 %copy-start.12 = (f32[2048]{0:T(1024)S(1)}, f32[2048]{0:T(1024)}, u32[]{:S(2)}) copy-start(f32[2048]{0:T(1024)} %copy-done.11) | copy-start | bytes 24580
  249.2 24.6 %copy-start = (bf16[1,2048,1024]{1,2,0:T(8,128)(2,1)S(1)}, bf16[1,2048,1024]{1,2,0:T(8,128)(2,1)}, u32[]{:S(2)}) copy-start(bf16[1,2048,1024]{1,2,0:T(8,128)(2,1)} %copy.21) | copy-start | bytes 12582916
  249.2 24.6 %copy-start.3 = (bf16[2048,1024]{0,1:T(8,128)(2,1)S(1)}, bf16[2048,1024]{0,1:T(8,128)(2,1)}, u32[]{:S(2)}) copy-start(bf16[2048,1024]{0,1:T(8,128)(2,1)} %copy-done.2) | copy-start | bytes 12582916
  278.5 25.2 %copy-start.14 = (f32[2048]{0:T(1024)S(1)}, f32[2048]{0:T(1024)}, u32[]{:S(2)}) copy-start(f32[2048]{0:T(1024)} %copy-done.13) | copy-start | bytes 24580
  339.6 213.1 %reduce-scatter.11.cloned.1.call-start = ((), (), s32[]{:S(2)}) async-start(), calls=%async_computation.8 | async-start | bytes 8912896 | tf_op jit(solution)/shard_map/reduce_scatter | solution.py:46
  366.4 0.7 copy-start.10
  366.4 293.4 %reduce-scatter.13.cloned.1.call-start = ((), (), s32[]{:S(2)}) async-start(), calls=%async_computation.9 | async-start | bytes 8912896 | tf_op jit(solution)/shard_map/reduce_scatter | solution.py:46
  390.1 377.0 %reduce-scatter.15.cloned.1.call-start = ((), (), s32[]{:S(2)}) async-start(), calls=%async_computation.10 | async-start | bytes 8912896 | tf_op jit(solution)/shard_map/reduce_scatter | solution.py:46
  414.2 460.1 %reduce-scatter.17.cloned.1.call-start = ((), (), s32[]{:S(2)}) async-start(), calls=%async_computation.11 | async-start | bytes 8912896 | tf_op jit(solution)/shard_map/reduce_scatter | solution.py:46
  445.1 467.0 %copy-start.4 = (f32[2,256,1024]{2,1,0:T(8,128)S(1)}, f32[2,256,1024]{2,1,0:T(8,128)}, u32[]{:S(2)}) copy-start(f32[2,256,1024]{2,1,0:T(8,128)} %param.21) | copy-start | bytes 6291460
  445.1 595.1 %all-gather.8.cloned.1.call-start = ((), (), s32[]{:S(2)}) async-start(), calls=%async_computation.14 | async-start | bytes 17825792 | tf_op jit(solution)/shard_map/all_gather | solution.py:79
  909.7 7.4 copy-start.8
  917.1 250.4 %all-gather.6.cloned.1.call-start = ((), (), s32[]{:S(2)}) async-start(), calls=%async_computation.13 | async-start | bytes 17825792 | tf_op jit(solution)/shard_map/all_gather | solution.py:79
  917.2 7.0 copy-start.6
  917.3 7.0 copy-start.7
  918.5 5.9 copy-start.5
  924.1 370.6 %all-gather.4.cloned.1.call-start = ((), (), s32[]{:S(2)}) async-start(), calls=%async_computation.12 | async-start | bytes 17825792 | tf_op jit(solution)/shard_map/all_gather | solution.py:79
  1294.7 16.8 %copy-start.1 = (bf16[2,1024,4096]{2,1,0:T(8,128)(2,1)S(1)}, bf16[2,1024,4096]{2,1,0:T(8,128)(2,1)}, u32[]{:S(2)}) copy-start(bf16[2,1024,4096]{2,1,0:T(8,128)(2,1)} %all-gather.6.cloned.1.call-done) | copy-start | bytes 50331652
  1294.7 25.3 %slice-start = ((s8[16777216]{0:T(1024)(128)(4,1)}), s8[4194304]{0:T(1024)(128)(4,1)S(1)}, s32[]{:S(2)}) async-start(s8[16777216]{0:T(1024)(128)(4,1)} %bitcast.81), calls=%async_computation.15 | async-start | bytes 8388608
  1294.7 25.3 %slice-start.1 = ((s8[16777216]{0:T(1024)(128)(4,1)}), s8[4194304]{0:T(1024)(128)(4,1)S(1)}, s32[]{:S(2)}) async-start(s8[16777216]{0:T(1024)(128)(4,1)} %bitcast.81), calls=%async_computation.16 | async-start | bytes 8388608
  1311.5 9.9 slice-start.2
  1311.5 11.1 slice-start.3
Sparse Core Ops, SparseCore 0:
  218.8 106.0 reduce-scatter.8
  339.7 106.0 reduce-scatter.6
  449.8 102.7 reduce-scatter.10
  557.1 102.6 reduce-scatter.12
  664.3 102.6 reduce-scatter.14
  771.6 102.6 reduce-scatter.16
  917.2 122.9 all-gather.7
  1043.0 124.3 all-gather.5
  1170.3 124.3 all-gather.3

commit v2 on v1

--- a/solution.py
+++ b/solution.py
@@ -1,10 +1,15 @@
+import functools
+
 import jax
 import jax.numpy as jnp
 from jax import lax
+from jax.experimental import pallas as pl
+from jax.experimental.pallas import tpu as pltpu
 from jax.sharding import PartitionSpec as P
 
 NAMES = ("w_gate", "w_up", "w_down")
 F32, BF16 = jnp.float32, jnp.bfloat16
+MESH = pl.DeviceIdType.MESH
 
 
 def dot(a, b, ca, cb):
@@ -33,6 +38,98 @@
     v = 0.95 * v + 0.05 * g * g
     step = m * lax.rsqrt(v + 1e-8) + 0.1 * w
     return (w - 0.02 * step).astype(BF16), m, v
+
+
+def place(n):
+    me = lax.axis_index("dp")
+    core, chip = me % 2, me // 2
+    half = n // 4
+    pos = chip + (chip // half) * (3 * half - 1 - 2 * chip)
+
+    def owner(p, c):
+        return 2 * (p + (p // half) * (3 * half - 1 - 2 * p)) + c
+
+    return core, pos, owner
+
+
+def entry_barrier(devices):
+    sem = pltpu.get_barrier_semaphore()
+    for d in devices:
+        pl.semaphore_signal(sem, inc=1, device_id={"dp": d}, device_id_type=MESH)
+    pl.semaphore_wait(sem, len(devices))
+
+
+def remote(src, dst, send, recv, dev):
+    return pltpu.make_async_remote_copy(
+        src_ref=src, dst_ref=dst, send_sem=send, recv_sem=recv, device_id={"dp": dev}, device_id_type=MESH
+    )
+
+
+def gather_kernel(n, rows, *refs):
+    k = len(rows)
+    ins, outs, bufs = refs[:k], refs[k : 2 * k], refs[2 * k : 3 * k]
+    ring_send, ring_recv, d2d_send, d2d_recv, local = refs[3 * k :]
+    chips = n // 2
+    core, pos, owner = place(n)
+    right, left = owner((pos + 1) % chips, core), owner((pos + chips - 1) % chips, core)
+    partner = owner(pos, 1 - core)
+    entry_barrier((left, right, partner))
+    to = (right, left)
+
+    def out_rows(i, way, s, c):
+        q = (pos + (chips - s if way == 0 else s)) % chips
+        h = rows[i] // 2
+        return outs[i].at[:, pl.ds(pl.multiple_of(owner(q, c) * rows[i] + way * h, h), h)]
+
+    def hop(i, way, s):
+        return remote(bufs[i].at[way, s], bufs[i].at[way, s + 1], ring_send.at[i, way, s], ring_recv.at[i, way, s], to[way])
+
+    def across(i, way, s, c):
+        return remote(bufs[i].at[way, s], out_rows(i, way, s, c), d2d_send.at[i, way, s], d2d_recv.at[i, way, s], partner)
+
+    def keep(i, way, s):
+        return pltpu.make_async_copy(bufs[i].at[way, s], out_rows(i, way, s, core), local.at[i, way, s])
+
+    def load(i, way):
+        h = rows[i] // 2
+        return pltpu.make_async_copy(ins[i].at[:, pl.ds(way * h, h)], bufs[i].at[way, 0], local.at[i, way, chips])
+
+    every = [(i, way) for i in range(k) for way in range(2)]
+    for i, way in every:
+        load(i, way).start()
+    for s in range(chips):
+        for i, way in every:
+            if s == 0:
+                load(i, way).wait()
+            else:
+                hop(i, way, s - 1).wait_recv()
+            if s < chips - 1:
+                hop(i, way, s).start()
+            across(i, way, s, core).start()
+            keep(i, way, s).start()
+    for s in range(chips):
+        for i, way in every:
+            if s < chips - 1:
+                hop(i, way, s).wait_send()
+            across(i, way, s, core).wait_send()
+            across(i, way, s, 1 - core).wait_recv()
+            keep(i, way, s).wait()
+
+
+def gather(n, blocks, collective_id):
+    k, chips = len(blocks), n // 2
+    rows = [b.shape[1] for b in blocks]
+    sems = [pltpu.SemaphoreType.DMA((k, 2, chips))] * 4 + [pltpu.SemaphoreType.DMA((k, 2, chips + 1))]
+    sent = 2 * sum(b.size * 2 for b in blocks) * (chips - 1)
+    return pl.pallas_call(
+        functools.partial(gather_kernel, n, rows),
+        out_shape=[jax.ShapeDtypeStruct((b.shape[0], n * b.shape[1], b.shape[2]), b.dtype) for b in blocks],
+        in_specs=[pl.BlockSpec(memory_space=pl.ANY)] * k,
+        out_specs=[pl.BlockSpec(memory_space=pl.ANY)] * k,
+        scratch_shapes=[pltpu.VMEM((2, chips, b.shape[0], b.shape[1] // 2, b.shape[2]), b.dtype) for b in blocks] + sems,
+        compiler_params=pltpu.CompilerParams(collective_id=collective_id, has_side_effects=True, vmem_limit_bytes=60 << 20),
+        name="gather_weights",
+    )(*blocks)
 
 
 def solution(mesh):
@@ -76,10 +173,10 @@
             own = lax.dynamic_slice_in_dim(w, me * rows, rows, 1)
             g = jnp.stack([p.astype(F32) for p in pair]) * factor
             new, nm, nv = adamw(own.astype(F32), mm, vv, g)
-            news.append(lax.all_gather(new, "dp", axis=1, tiled=True))
+            news.append(new)
             ms.append(nm)
             vs.append(nv)
-        return (*news, *ms, *vs)
+        return (*gather(n, news, 0), *ms, *vs)
 
     seq, whole, shard = P(("rep", "dp")), P(), P(None, "dp")
     return jax.shard_map(

time: 1340 us -> 1220 us (0.910)
  waiting for transfers between devices: 782 us -> 416 us
  Pallas kernels: 0 us -> 243 us
    all_gather x3 -> x0, waiting for transfers between devices: 366 us -> none  [body(): news.append(lax.all_gather(new, 'dp', axis=1, tiled=True))]
    pallas_call x0 -> x1, Pallas kernels: none -> 243 us  [gather(): pl.pallas_call(functools.partial(gather_kernel, n, rows), out_shape=[jax....]
    unnamed x43 -> x51, local copies, waits for them, and re-layouts: 47.7 us -> 48.5 us
  transfers between devices with their start and end apart: 9 -> 6, of which waited for: 7 -> 4; matrix products, arithmetic and copies ran while one was open for 18% -> 19% of each run, Pallas kernels for 0% -> 0%
where the time goes in v2:
time: 1220 us; the launch traced here: 1210 us
  matrix products  416 us (34%)
  waiting for transfers between devices  416 us (34%)
  Pallas kernels  243 us (20%)
  local copies, waits for them, and re-layouts  48.5 us (4%)
  other arithmetic  33.7 us (3%)
  blocking collectives  32.2 us (3%)
  between operations  19.5 us (2%)
    reduce_scatter x6, waiting for transfers between devices, scatter(): return lax.psum_scatter(g, 'dp', scatter_dimension=0, tiled=True)  416 us
    dot_general x15, matrix products, dot(): lax.dot_general(a, b, (((ca,), (cb,)), ((), ())), preferred_element_type=...  416 us
    pallas_call x1, Pallas kernels, gather(): pl.pallas_call(functools.partial(gather_kernel, n, rows), out_shape=[jax....  243 us
    unnamed x51, local copies, waits for them, and re-layouts  48.5 us
    psum x1, blocking collectives, body(): total = lax.psum(total, 'dp')  32.2 us
  transfers between devices with their start and end apart: 6, of which 4 were waited for; matrix products, arithmetic and copies ran while one was open for 19% of the time, Pallas kernels for 0%

profile of v2, /device:TPU:0, one launch (start us, length us, event | category | flops | bytes accessed | tf_op | source)
XLA Modules:
  0.0 1209.6 jit_solution(17162646932787711506)
XLA Ops:
  7.2 6.5 copy.20
  13.7 3.1 fusion.13
  16.8 24.4 %fusion.33 = f32[2048,4096]{1,0:T(8,128)} fusion(bf16[2,1024,4096]{2,1,0:T(8,128)(2,1)} %param.13, bf16[1,2048,1024]{2,1,0:T(8,128)(2,1)} %param.11, f32[2048]{0:T(1024)S(1)} %add_rsqrt_fusion), kind=kOutput, calls=%fused_computation.48 | convolution fusion | flops 17186160640 | bytes 46145536 | tf_op jit(solution)/shard_map/dot_general | solution.py:16
  41.2 38.1 %multiply_convert_fusion.1 = (bf16[2048,4096]{1,0:T(8,128)(2,1)}, f32[2048,4096]{1,0:T(8,128)}) fusion(f32[2048,4096]{1,0:T(8,128)} %fusion.33, bf16[2,1024,4096]{2,1,0:T(8,128)(2,1)} %param.14, bf16[1,2048,1024]{2,1,0:T(8,128)(2,1)} %param.11, f32[2048]{0:T(1024)S(1)} %add_rsqrt_fusion), kind=kOutput, calls=%fused_computation.13 | convolution fusion | flops 17236492288 | bytes 96477184 | tf_op jit(solution)/shard_map/dot_general | solution.py:16
  79.3 24.0 %fusion.17 = (f32[2048]{0:T(1024)S(1)}, bf16[2048,1024]{0,1:T(8,128)(2,1)S(1)}) fusion(bf16[2048,4096]{1,0:T(8,128)(2,1)} %get-tuple-element.26, bf16[2,4096,1024]{2,1,0:T(8,128)(2,1)} %param.15, bf16[1,2048,1024]{1,2,0:T(8,128)(2,1)} %copy.20), kind=kOutput, calls=%fused_computation.32 | convolution fusion | flops 17190352896 | bytes 33562624 | tf_op jit(solution)/shard_map/dot_general | solution.py:16
  103.4 24.8 %fusion.26 = f32[2048,4096]{1,0:T(8,128)} fusion(bf16[2,1024,4096]{2,1,0:T(8,128)(2,1)} %param.14, bf16[2048,1024]{0,1:T(8,128)(2,1)S(1)} %get-tuple-element.29, f32[2048]{0:T(1024)S(1)} %fusion.88), kind=kOutput, calls=%fused_computation.41 | convolution fusion | flops 17186160640 | bytes 46145536 | tf_op jit(solution)/shard_map/dot_general | solution.py:16
  128.1 23.4 %fusion.22 = f32[2048,4096]{1,0:T(8,128)} fusion(bf16[2,1024,4096]{2,1,0:T(8,128)(2,1)} %param.13, bf16[2048,1024]{0,1:T(8,128)(2,1)S(1)} %get-tuple-element.29, f32[2048]{0:T(1024)S(1)} %fusion.88), kind=kOutput, calls=%fused_computation.37 | convolution fusion | flops 17186160640 | bytes 46145536 | tf_op jit(solution)/shard_map/dot_general | solution.py:16
  151.6 44.3 %fusion.2 = (bf16[2048,4096]{1,0:T(8,128)(2,1)}, bf16[2048,4096]{1,0:T(8,128)(2,1)}) fusion(f32[2048,4096]{1,0:T(8,128)} %fusion.22, f32[2048,4096]{1,0:T(8,128)} %fusion.26, bf16[2,4096,1024]{2,1,0:T(8,128)(2,1)} %param.15, bf16[1,2048,1024]{2,1,0:T(8,128)(2,1)} %param.12), kind=kOutput, calls=%fused_computation.6 | convolution fusion | flops 17305698304 | bytes 113246208 | tf_op jit(solution)/shard_map/dot_general | solution.py:16
  195.9 22.9 %convolution_convert_fusion.4 = bf16[1024,4096]{1,0:T(8,128)(2,1)} fusion(bf16[2048,4096]{1,0:T(8,128)(2,1)} %get-tuple-element.25, bf16[2048,1024]{0,1:T(8,128)(2,1)} %copy-done.2, f32[2048]{0:T(1024)S(1)} %fusion.88), kind=kOutput, calls=%fused_computation.60 | convolution fusion | flops 17190354944 | bytes 29368320 | tf_op jit(solution)/shard_map/dot_general | solution.py:16
  218.8 0.0 reduce-scatter.7.cloned.1.call-start
  218.9 24.0 %fusion.20 = bf16[2048,1024]{0,1:T(8,128)(2,1)} fusion(bf16[2048,4096]{1,0:T(8,128)(2,1)} %get-tuple-element.25, bf16[2,1024,4096]{2,1,0:T(8,128)(2,1)} %param.13), kind=kOutput, calls=%fused_computation.35 | convolution fusion | flops 17179869184 | bytes 29360128 | tf_op jit(solution)/shard_map/dot_general | solution.py:16
  242.9 6.4 copy.21
  249.3 24.5 %fusion.19 = (f32[2048]{0:T(1024)S(1)}, bf16[2048,1024]{0,1:T(8,128)(2,1)S(1)}) fusion(bf16[2048,1024]{0,1:T(8,128)(2,1)} %copy-done.2, bf16[2048,1024]{0,1:T(8,128)(2,1)} %fusion.20, bf16[2048,4096]{1,0:T(8,128)(2,1)} %get-tuple-element.24, bf16[2,1024,4096]{2,1,0:T(8,128)(2,1)} %param.14), kind=kOutput, calls=%fused_computation.34 | convolution fusion | flops 17192450048 | bytes 37756928 | tf_op jit(solution)/shard_map/dot_general | solution.py:16
  273.9 4.7 fusion.55
  278.6 25.2 %convolution_convert_fusion = bf16[2048,4096]{1,0:T(8,128)(2,1)} fusion(bf16[2048,1024]{0,1:T(8,128)(2,1)} %fusion.55, bf16[2,4096,1024]{2,1,0:T(8,128)(2,1)} %param.15), kind=kOutput, calls=%fused_computation.19 | convolution fusion | flops 17188257792 | bytes 29360128 | tf_op jit(solution)/shard_map/dot_general | solution.py:16
  303.8 35.9 %fusion.39 = bf16[1024,4096]{1,0:T(8,128)(2,1)} fusion(f32[2048,4096]{1,0:T(8,128)} %get-tuple-element.27, bf16[2048,4096]{1,0:T(8,128)(2,1)} %convolution_convert_fusion, f32[2048,4096]{1,0:T(8,128)} %fusion.33, bf16[1,2048,1024]{1,2,0:T(8,128)(2,1)} %copy.20, f32[2048]{0:T(1024)S(1)} %copy-done.18), kind=kOutput, calls=%fused_computation.55 | convolution fusion | flops 17282629632 | bytes 96477184 | tf_op jit(solution)/shard_map/dot_general | solution.py:16
  339.8 26.7 %fusion.42 = bf16[1024,4096]{1,0:T(8,128)(2,1)} fusion(bf16[2048,4096]{1,0:T(8,128)(2,1)} %convolution_convert_fusion, f32[2048,4096]{1,0:T(8,128)} %fusion.33, bf16[1,2048,1024]{1,2,0:T(8,128)(2,1)} %copy.20, f32[2048]{0:T(1024)S(1)} %copy-done.18), kind=kOutput, calls=%fused_computation.56 | convolution fusion | flops 17249075200 | bytes 62922752 | tf_op jit(solution)/shard_map/dot_general | solution.py:16
  366.6 0.0 reduce-scatter.13.cloned.1.call-start
  366.6 0.6 copy-done.14
  367.3 23.0 %convolution_convert_fusion.3 = bf16[1024,4096]{1,0:T(8,128)(2,1)} fusion(bf16[2048,4096]{1,0:T(8,128)(2,1)} %get-tuple-element.24, bf16[2048,1024]{0,1:T(8,128)(2,1)} %copy-done.2, f32[2048]{0:T(1024)S(1)} %copy-done.14), kind=kOutput, calls=%fused_computation.59 | convolution fusion | flops 17190354944 | bytes 29368320 | tf_op jit(solution)/shard_map/dot_general | solution.py:16
  390.3 24.1 %convolution_convert_fusion.2 = bf16[4096,1024]{1,0:T(8,128)(2,1)} fusion(bf16[2048,4096]{1,0:T(8,128)(2,1)} %get-tuple-element.26, bf16[2048,1024]{0,1:T(8,128)(2,1)} %fusion.55), kind=kOutput, calls=%fused_computation.58 | convolution fusion | flops 17184063488 | bytes 29360128 | tf_op jit(solution)/shard_map/dot_general | solution.py:16
  414.5 30.8 %fusion.45 = bf16[4096,1024]{1,0:T(8,128)(2,1)} fusion(f32[2048,4096]{1,0:T(8,128)} %fusion.26, f32[2048,4096]{1,0:T(8,128)} %fusion.22, bf16[1,2048,1024]{2,1,0:T(8,128)(2,1)} %param.12), kind=kOutput, calls=%fused_computation.57 | convolution fusion | flops 17234395136 | bytes 79691776 | tf_op jit(solution)/shard_map/dot_general | solution.py:16
  445.3 2.1 fusion.83
  447.4 1.9 fusion.82
  450.6 102.2 %reduce-scatter.11.cloned.1.call-done = bf16[64,4096]{1,0:T(8,128)(2,1)} async-done(((bf16[1024,4096]{1,0:T(8,128)(2,1)}), bf16[64,4096]{1,0:T(8,128)(2,1)}) %reduce-scatter.11.cloned.1.call-update) | async-done | bytes 524304 | tf_op jit(solution)/shard_map/reduce_scatter | solution.py:143
  552.8 1.9 fusion.84
  555.3 104.7 %reduce-scatter.13.cloned.1.call-done = bf16[64,4096]{1,0:T(8,128)(2,1)} async-done(((bf16[1024,4096]{1,0:T(8,128)(2,1)}), bf16[64,4096]{1,0:T(8,128)(2,1)}) %reduce-scatter.13.cloned.1.call-update) | async-done | bytes 524304 | tf_op jit(solution)/shard_map/reduce_scatter | solution.py:143
  660.0 1.9 fusion.85
  662.6 104.6 %reduce-scatter.15.cloned.1.call-done = bf16[256,1024]{1,0:T(8,128)(2,1)} async-done(((bf16[4096,1024]{1,0:T(8,128)(2,1)}), bf16[256,1024]{1,0:T(8,128)(2,1)}) %reduce-scatter.15.cloned.1.call-update) | async-done | bytes 524304 | tf_op jit(solution)/shard_map/reduce_scatter | solution.py:143
  767.2 1.9 fusion.86
  769.8 104.7 %reduce-scatter.17.cloned.1.call-done = bf16[256,1024]{1,0:T(8,128)(2,1)} async-done(((bf16[4096,1024]{1,0:T(8,128)(2,1)}), bf16[256,1024]{1,0:T(8,128)(2,1)}) %reduce-scatter.17.cloned.1.call-update) | async-done | bytes 524304 | tf_op jit(solution)/shard_map/reduce_scatter | solution.py:143
  874.4 1.9 fusion.87
  877.0 32.2 %psum.7 = f32[]{:T(128)} all-reduce(f32[]{:T(128)S(6)} %add.134), channel_id=1, replica_groups=mesh['rep'=2,'dp'=16] {'dp'}, use_global_device_ids=true, to_apply=%region_15.16 | all-reduce | flops 1 | bytes 8 | tf_op jit(solution)/shard_map/psum | solution.py:166
  909.9 1.2 convert_bitcast_fusion.1
  911.1 1.2 convert_bitcast_fusion
  912.4 5.2 fusion.76
  917.6 0.1 convert_bitcast_fusion.2
  917.7 0.1 convert_bitcast_fusion.3
  917.8 0.1 convert_bitcast_fusion.4
  917.9 0.1 convert_bitcast_fusion.5
  918.0 0.8 copy-done.8
  918.8 6.3 fusion.70
  925.1 243.1 %gather_weights.1 = (bf16[2,1024,4096]{2,1,0:T(8,128)(2,1)}, bf16[2,1024,4096]{2,1,0:T(8,128)(2,1)}, bf16[2,4096,1024]{2,1,0:T(8,128)(2,1)}) custom-call(bf16[2,64,4096]{2,1,0:T(8,128)(2,1)} %get-tuple-element.21.refs_0_, bf16[2,64,4096]{2,1,0:T(8,128)(2,1)} %get-tuple-element.32.refs_1_, bf16[2,256,1024]{2,1,0:T(8,128)(2,1)} %get-tuple-element.15.refs_2_), custom_call_target="tpu_custom_call" | custom-call | tf_op jit(solution)/shard_map/gather_weights/pallas_call | solution.py:124
  1168.2 16.8 %copy.25 = bf16[2,1024,4096]{2,1,0:T(8,128)(2,1)} copy(bf16[2,1024,4096]{2,1,0:T(8,128)(2,1)} %get-tuple-element.44) | data formatting | bytes 33554432
  1185.0 8.5 copy.26
  1193.6 1.4 slice-done.2
  1195.0 1.2 slice-done.3
  1196.2 6.2 copy.27
  (58 shorter events, 0.4 us)
Async XLA Ops:
  7.2 438.1 %reduce-scatter.9.cloned.1.call-start = ((), (), s32[]{:S(2)}) async-start(), calls=%async_computation.7 | async-start | bytes 8912896 | tf_op jit(solution)/shard_map/reduce_scatter | solution.py:143
  16.8 24.4 %copy-start.17 = (f32[2048]{0:T(1024)}, f32[2048]{0:T(1024)S(1)}, u32[]{:S(2)}) copy-start(f32[2048]{0:T(1024)S(1)} %add_rsqrt_fusion) | copy-start | bytes 24580
  103.3 24.8 %copy-start.2 = (bf16[2048,1024]{0,1:T(8,128)(2,1)}, bf16[2048,1024]{0,1:T(8,128)(2,1)S(1)}, u32[]{:S(2)}) copy-start(bf16[2048,1024]{0,1:T(8,128)(2,1)S(1)} %get-tuple-element.29) | copy-start | bytes 12582916
  103.3 24.8 %copy-start.15 = (f32[2048]{0:T(1024)}, f32[2048]{0:T(1024)S(1)}, u32[]{:S(2)}) copy-start(f32[2048]{0:T(1024)S(1)} %get-tuple-element.28) | copy-start | bytes 24580
  103.4 170.5 %copy-start.13 = (f32[2048]{0:T(1024)}, f32[2048]{0:T(1024)S(1)}, u32[]{:S(2)}) copy-start(f32[2048]{0:T(1024)S(1)} %fusion.88) | copy-start | bytes 24580
  218.8 228.6 %reduce-scatter.7.cloned.1.call-start = ((), (), s32[]{:S(2)}) async-start(), calls=%async_computation.6 | async-start | bytes 8912896 | tf_op jit(solution)/shard_map/reduce_scatter | solution.py:143
  249.3 24.5 %copy-start.16 = (f32[2048]{0:T(1024)S(1)}, f32[2048]{0:T(1024)}, u32[]{:S(2)}) copy-start(f32[2048]{0:T(1024)} %copy-done.15) | copy-start | bytes 24580
  249.3 24.6 %copy-start = (bf16[1,2048,1024]{1,2,0:T(8,128)(2,1)S(1)}, bf16[1,2048,1024]{1,2,0:T(8,128)(2,1)}, u32[]{:S(2)}) copy-start(bf16[1,2048,1024]{1,2,0:T(8,128)(2,1)} %copy.21) | copy-start | bytes 12582916
  249.3 24.6 %copy-start.3 = (bf16[2048,1024]{0,1:T(8,128)(2,1)S(1)}, bf16[2048,1024]{0,1:T(8,128)(2,1)}, u32[]{:S(2)}) copy-start(bf16[2048,1024]{0,1:T(8,128)(2,1)} %copy-done.2) | copy-start | bytes 12582916
  278.6 25.2 %copy-start.18 = (f32[2048]{0:T(1024)S(1)}, f32[2048]{0:T(1024)}, u32[]{:S(2)}) copy-start(f32[2048]{0:T(1024)} %copy-done.17) | copy-start | bytes 24580
  339.8 213.0 %reduce-scatter.11.cloned.1.call-start = ((), (), s32[]{:S(2)}) async-start(), calls=%async_computation.8 | async-start | bytes 8912896 | tf_op jit(solution)/shard_map/reduce_scatter | solution.py:143
  366.6 0.7 copy-start.14
  366.6 293.4 %reduce-scatter.13.cloned.1.call-start = ((), (), s32[]{:S(2)}) async-start(), calls=%async_computation.9 | async-start | bytes 8912896 | tf_op jit(solution)/shard_map/reduce_scatter | solution.py:143
  390.3 376.9 %reduce-scatter.15.cloned.1.call-start = ((), (), s32[]{:S(2)}) async-start(), calls=%async_computation.10 | async-start | bytes 8912896 | tf_op jit(solution)/shard_map/reduce_scatter | solution.py:143
  414.4 460.0 %reduce-scatter.17.cloned.1.call-start = ((), (), s32[]{:S(2)}) async-start(), calls=%async_computation.11 | async-start | bytes 8912896 | tf_op jit(solution)/shard_map/reduce_scatter | solution.py:143
  445.2 467.1 %copy-start.4 = (f32[2,256,1024]{2,1,0:T(8,128)S(1)}, f32[2,256,1024]{2,1,0:T(8,128)}, u32[]{:S(2)}) copy-start(f32[2,256,1024]{2,1,0:T(8,128)} %param.21) | copy-start | bytes 6291460
  662.6 255.1 %copy-start.12 = (bf16[64,4096]{1,0:T(8,128)(2,1)S(1)}, bf16[64,4096]{1,0:T(8,128)(2,1)}, u32[]{:S(2)}) copy-start(bf16[64,4096]{1,0:T(8,128)(2,1)} %reduce-scatter.13.cloned.1.call-done) | copy-start | bytes 1572868
  909.9 7.8 copy-start.11
  911.1 6.7 copy-start.9
  912.3 5.6 copy-start.10
  912.4 5.6 copy-start.5
  912.4 5.6 copy-start.6
  912.4 5.6 copy-start.7
  912.4 6.4 copy-start.8
  1168.2 16.8 %copy-start.1 = (bf16[2,1024,4096]{2,1,0:T(8,128)(2,1)S(1)}, bf16[2,1024,4096]{2,1,0:T(8,128)(2,1)}, u32[]{:S(2)}) copy-start(bf16[2,1024,4096]{2,1,0:T(8,128)(2,1)} %get-tuple-element.45) | copy-start | bytes 50331652
  1168.2 25.3 %slice-start = ((s8[16777216]{0:T(1024)(128)(4,1)}), s8[4194304]{0:T(1024)(128)(4,1)S(1)}, s32[]{:S(2)}) async-start(s8[16777216]{0:T(1024)(128)(4,1)} %bitcast.81), calls=%async_computation.12 | async-start | bytes 8388608
  1168.2 25.3 %slice-start.1 = ((s8[16777216]{0:T(1024)(128)(4,1)}), s8[4194304]{0:T(1024)(128)(4,1)S(1)}, s32[]{:S(2)}) async-start(s8[16777216]{0:T(1024)(128)(4,1)} %bitcast.81), calls=%async_computation.13 | async-start | bytes 8388608
  1185.0 9.9 slice-start.2
  1185.0 11.1 slice-start.3
Sparse Core Ops, SparseCore 0:
  218.9 105.9 reduce-scatter.8
  339.9 106.0 reduce-scatter.6
  450.0 102.6 reduce-scatter.10
  557.2 102.6 reduce-scatter.12
  664.5 102.6 reduce-scatter.14
  771.7 102.6 reduce-scatter.16

commit v3 on v2

--- a/solution.py
+++ b/solution.py
@@ -7,9 +7,9 @@
 from jax.experimental.pallas import tpu as pltpu
 from jax.sharding import PartitionSpec as P
 
-NAMES = ("w_gate", "w_up", "w_down")
 F32, BF16 = jnp.float32, jnp.bfloat16
 MESH = pl.DeviceIdType.MESH
+TILE = 512
 
 
 def dot(a, b, ca, cb):
@@ -120,7 +120,6 @@
     k, chips = len(blocks), n // 2
     rows = [b.shape[1] for b in blocks]
     sems = [pltpu.SemaphoreType.DMA((k, 2, chips))] * 4 + [pltpu.SemaphoreType.DMA((k, 2, chips + 1))]
-    sent = 2 * sum(b.size * 2 for b in blocks) * (chips - 1)
     return pl.pallas_call(
         functools.partial(gather_kernel, n, rows),
         out_shape=[jax.ShapeDtypeStruct((b.shape[0], n * b.shape[1], b.shape[2]), b.dtype) for b in blocks],
@@ -132,6 +131,199 @@
     )(*blocks)
 
 
+def summed(refs, cols, step=512):
+    total = refs[0][:, pl.ds(cols, step)].astype(F32)
+    for r in refs[1:]:
+        total += r[:, pl.ds(cols, step)].astype(F32)
+    return total
+
+
+def last_kernel(n, refs_in, refs_out, own, made, tiles, got, buf, sems):
+    down, a_t, *by_hidden = refs_in
+    own_sem, d2d_send, d2d_recv, ring_send, ring_recv, tile_sem = sems
+    chips, k = n // 2, 3
+    grads = (down, made.at[0], made.at[1])
+    rows = [g.shape[0] // n for g in grads]
+    wide = [g.shape[1] // 2 for g in grads]
+    core, pos, owner = place(n)
+    right, left = owner((pos + 1) % chips, core), owner((pos + chips - 1) % chips, core)
+    partner = owner(pos, 1 - core)
+    entry_barrier((left, right, partner))
+    to = (right, left)
+
+    def start_row(i, d, c, more=0):
+        at = owner((pos + d) % chips, c) * rows[i] + more
+        return pl.multiple_of(at, rows[i] // 2)
+
+    def load(d):
+        return pltpu.make_async_copy(down.at[pl.ds(start_row(0, d, core), rows[0])], own.at[d], own_sem.at[d])
+
+    def cross(i, d):
+        src = grads[i].at[pl.ds(start_row(i, d, 1 - core), rows[i])]
+        return remote(src, got[i].at[d], d2d_send.at[i, d], d2d_recv.at[i, d], partner)
+
+    def hop(i, part, way, s):
+        cols = pl.ds(part * wide[i], wide[i])
+        return remote(
+            buf[i].at[way, s, :, cols],
+            buf[i].at[way, s + 1, :, cols],
+            ring_send.at[i, part, way, s],
+            ring_recv.at[i, part, way, s],
+            to[way],
+        )
+
+    order = list(dict.fromkeys(d % chips for s in range(chips) for d in (chips - 1 - s, 1 + s)))
+
+    def begin(i):
+        for d in order:
+            cross(i, d).start()
+            if i == 0:
+                load(d).start()
+
+    ready = set()
+
+    def turn(i, number):
+        part, s = number % 2, number // 2
+        h = rows[i] // 2
+        for way in range(2):
+            d = (chips - 1 - s if way == 0 else 1 + s) % chips
+            if (i, d) not in ready:
+                ready.add((i, d))
+                if i == 0:
+                    load(d).wait()
+                cross(i, d).wait_recv()
+            if s > 0:
+                hop(i, part, way, s - 1).wait_recv()
+            half = pl.ds(way * h, h)
+            mine = own.at[d, half] if i == 0 else grads[i].at[pl.ds(start_row(i, d, core, way * h), h)]
+            terms = [mine, got[i].at[d, half]] + ([buf[i].at[way, s]] if s > 0 else [])
+            result = buf[i].at[way, s] if s < chips - 1 else refs_out[i].at[half]
+
+            def add(c, _, terms=terms, result=result, part=part, i=i):
+                at = pl.multiple_of(part * wide[i] + c * 512, 512)
+                result[:, pl.ds(at, 512)] = summed(terms, at).astype(BF16)
+                return 0
+
+            lax.fori_loop(0, wide[i] // 512, add, 0)
+            if s < chips - 1:
+                hop(i, part, way, s).start()
+
+    per = by_hidden[0].shape[1] // TILE
+    count = 2 * per
+
+    def fetch(t):
+        src = by_hidden[t // per].at[:, pl.ds(t % per * TILE, TILE)]
+        return pltpu.make_async_copy(src, tiles.at[t % 2], tile_sem.at[t % 2])
+
+    high = min(512, a_t.shape[0])
+    begin(0)
+    fetch(0).start()
+    gate, up = list(range(2 * chips)), list(range(2 * chips))
+    for t in range(count):
+        fetch(t).wait()
+        if t + 1 < count:
+            fetch(t + 1).start()
+
+        def matmul(m, _, t=t):
+            at = pl.ds(pl.multiple_of(m * high, high), high)
+            made[t // per, at, pl.ds(t % per * TILE, TILE)] = jnp.dot(
+                a_t[at], tiles[t % 2], preferred_element_type=F32
+            ).astype(BF16)
+            return 0
+
+        lax.fori_loop(0, a_t.shape[0] // high, matmul, 0)
+        for number in range(t * 2 * chips // count, (t + 1) * 2 * chips // count):
+            turn(0, number)
+        if t == per - 1:
+            begin(1)
+        if t > per:
+            turn(1, gate.pop(0))
+    begin(2)
+    while gate or up:
+        if gate:
+            turn(1, gate.pop(0))
+        if up:
+            turn(2, up.pop(0))
+    for i in range(k):
+        for d in range(chips):
+            cross(i, d).wait_send()
+        for part in range(2):
+            for way in range(2):
+                for s in range(chips - 1):
+                    hop(i, part, way, s).wait_send()
+
+
+def last_gradients(n, down, a_t, by_gate, by_up, collective_id):
+    chips, k = n // 2, 3
+    shapes = [down.shape, (a_t.shape[0], by_gate.shape[1]), (a_t.shape[0], by_up.shape[1])]
+    rows = [s[0] // n for s in shapes]
+    dma = pltpu.SemaphoreType.DMA
+    scratch = (
+        [pltpu.VMEM((chips, rows[0], shapes[0][1]), BF16), pltpu.VMEM((2, *shapes[1]), BF16), pltpu.VMEM((2, a_t.shape[1], TILE), BF16)]
+        + [pltpu.VMEM((chips, r, s[1]), BF16) for r, s in zip(rows, shapes)]
+        + [pltpu.VMEM((2, chips, r // 2, s[1]), BF16) for r, s in zip(rows, shapes)]
+        + [dma((chips,))]
+        + [dma((k, chips))] * 2
+        + [dma((k, 2, 2, chips - 1))] * 2
+        + [dma((2,))]
+    )
+
+    def kernel(*refs):
+        own, made, tiles = refs[7:10]
+        last_kernel(n, refs[:4], refs[4:7], own, made, tiles, refs[10:13], refs[13:16], refs[16:])
+
+    hbm, vmem = pl.BlockSpec(memory_space=pl.ANY), pl.BlockSpec(memory_space=pltpu.VMEM)
+    return pl.pallas_call(
+        kernel,
+        out_shape=[jax.ShapeDtypeStruct((r, s[1]), BF16) for r, s in zip(rows, shapes)],
+        in_specs=[hbm, vmem, hbm, hbm],
+        out_specs=[vmem] * k,
+        scratch_shapes=scratch,
+        compiler_params=pltpu.CompilerParams(collective_id=collective_id, has_side_effects=True, vmem_limit_bytes=62 << 20),
+        name="last_gradients",
+    )(down, a_t, by_gate, by_up)
+
+
+def square_kernel(n, *refs):
+    ins, out, slots, send, recv = refs[:-4], refs[-4], refs[-3], refs[-2], refs[-1]
+    me = lax.axis_index("dp")
+    others = [(me + j) % n for j in range(1, n)]
+    entry_barrier(others)
+    total = jnp.zeros((8, 512), F32)
+    for ref in ins:
+        rows, cols = ref.shape
+
+        def add(c, total, ref=ref, cols=cols):
+            row = pl.multiple_of(c // (cols // 512) * 16, 16)
+            g = ref[pl.ds(row, 16), pl.ds(pl.multiple_of(c % (cols // 512) * 512, 512), 512)].astype(F32)
+            return total + g[:8] * g[:8] + g[8:] * g[8:]
+
+        total = lax.fori_loop(0, rows // 16 * (cols // 512), add, total)
+    slots[0] = jnp.broadcast_to(jnp.sum(jnp.sum(total, 1, keepdims=True), 0, keepdims=True), (8, 128))
+    copies = [remote(slots.at[0], slots.at[j], send.at[j], recv.at[j], d) for j, d in enumerate(others, 1)]
+    for c in copies:
+        c.start()
+    for c in copies:
+        c.wait_send()
+        c.wait_recv()
+    total = slots[0]
+    for j in range(1, n):
+        total += slots[j]
+    out[...] = total
+
+
+def sum_of_squares(n, blocks, collective_id):
+    return pl.pallas_call(
+        functools.partial(square_kernel, n),
+        out_shape=jax.ShapeDtypeStruct((8, 128), F32),
+        in_specs=[pl.BlockSpec(memory_space=pltpu.VMEM)] * len(blocks),
+        out_specs=pl.BlockSpec(memory_space=pltpu.VMEM),
+        scratch_shapes=[pltpu.VMEM((n, 8, 128), F32)] + [pltpu.SemaphoreType.DMA((n,))] * 2,
+        compiler_params=pltpu.CompilerParams(collective_id=collective_id, has_side_effects=True),
+        name="sum_of_squares",
+    )(*blocks)[0, 0]
+
+
 def solution(mesh):
     n = mesh.shape["dp"]
 
@@ -139,7 +331,7 @@
         h0, dy = x[0], dy[0]
         m, v = mv[:3], mv[3:]
 
-        def scatter(g):
+        def scatter_by_xla(g):
             return lax.psum_scatter(g, "dp", scatter_dimension=0, tiled=True)
 
         a0 = normed(h0)
@@ -149,21 +341,25 @@
         a1, norm_back = jax.vjp(normed, h1)
         g1, u1 = dot(a1, wg[1], 1, 0), dot(a1, wu[1], 1, 0)
         hid1 = act(g1, u1)
-        d_down1 = scatter(dot(hid1, dy, 0, 0).astype(BF16))
+        grad = lambda a, b: dot(a, b, 0, 0).astype(BF16)
+        t_down1 = grad(hid1, dy)
+        d_down1 = scatter_by_xla(t_down1)
+        dy, _ = lax.optimization_barrier((dy, t_down1))
         dhid1 = dot(dy, wd[1], 1, 1).astype(BF16)
         dg1, du1 = act_back(g1, u1, dhid1)
-        d_gate1 = scatter(dot(a1, dg1, 0, 0).astype(BF16))
-        d_up1 = scatter(dot(a1, du1, 0, 0).astype(BF16))
+        t_gate1 = grad(a1, dg1)
+        d_gate1 = scatter_by_xla(t_gate1)
+        t_up1 = grad(a1, du1)
+        d_up1 = scatter_by_xla(t_up1)
+        dg1, du1, _, _ = lax.optimization_barrier((dg1, du1, t_gate1, t_up1))
         da1 = dot(dg1, wg[1], 1, 1).astype(BF16) + dot(du1, wu[1], 1, 1).astype(BF16)
         dh1 = dy + norm_back(da1)[0]
-        d_down0 = scatter(dot(hid0, dh1, 0, 0).astype(BF16))
+        t_down0 = grad(hid0, dh1)
         dhid0 = dot(dh1, wd[0], 1, 1).astype(BF16)
         dg0, du0 = act_back(g0, u0, dhid0)
-        d_gate0 = scatter(dot(a0, dg0, 0, 0).astype(BF16))
-        d_up0 = scatter(dot(a0, du0, 0, 0).astype(BF16))
+        d_down0, d_gate0, d_up0 = last_gradients(n, t_down0, a0.T, dg0, du0, 1)
         gs = [(d_gate0, d_gate1), (d_up0, d_up1), (d_down0, d_down1)]
-        total = sum(jnp.sum(jnp.square(g.astype(F32))) for pair in gs for g in pair)
-        total = lax.psum(total, "dp")
+        total = sum_of_squares(n, [g for pair in gs for g in pair], 2)
         count = sum(w.size for w in (wg, wu, wd))
         factor = jnp.minimum(1.0, 0.5 * lax.rsqrt(total / count + 1e-30))
         me = lax.axis_index("dp")

time: 1220 us -> 919 us (0.75)
  waiting for transfers between devices: 416 us -> 0.11 us
  Pallas kernels: 243 us -> 443 us
  matrix products: 416 us -> 378 us
  blocking collectives: 32.2 us -> 0 us
    reduce_scatter x6 -> x3, waiting for transfers between devices: 416 us -> 0.06 us  [scatter_by_xla(): return lax.psum_scatter(g, 'dp', scatter_dimension=0, tiled=True)]
    pallas_call x0 -> x2, Pallas kernels: none -> 198 us  [the longest x1 186 us: last_gradients(): pl.pallas_call(kernel, out_shape=[jax.ShapeDtypeStruct((r, s[1]), BF16) f...]
    dot_general x15 -> x13, matrix products: 416 us -> 378 us  [dot(): lax.dot_general(a, b, (((ca,), (cb,)), ((), ())), preferred_element_type=...]
    psum x1 -> x0, blocking collectives: 32.2 us -> none  [body(): total = lax.psum(total, 'dp')]
    unnamed x51 -> x49, local copies, waits for them, and re-layouts: 48.5 us -> 47.6 us
  transfers between devices with their start and end apart: 6 -> 3, of which waited for: 4 -> 0; matrix products, arithmetic and copies ran while one was open for 19% -> 25% of each run, Pallas kernels for 0% -> 20%
where the time goes in v3:
time: 919 us; the launch traced here: 911 us
  Pallas kernels  443 us (48%)
  matrix products  378 us (41%)
  local copies, waits for them, and re-layouts  48.9 us (5%)
  other arithmetic  26 us (3%)
  between operations  15.6 us (2%)
    dot_general x13, matrix products, dot(): lax.dot_general(a, b, (((ca,), (cb,)), ((), ())), preferred_element_type=...  378 us
    pallas_call x1, Pallas kernels, gather(): pl.pallas_call(functools.partial(gather_kernel, n, rows), out_shape=[jax....  244 us
    pallas_call x1, Pallas kernels, last_gradients(): pl.pallas_call(kernel, out_shape=[jax.ShapeDtypeStruct((r, s[1]), BF16) f...  186 us
    unnamed x49, local copies, waits for them, and re-layouts  47.6 us
  transfers between devices with their start and end apart: 3, of which 0 were waited for; matrix products, arithmetic and copies ran while one was open for 25% of the time, Pallas kernels for 20%

profile of v3, /device:TPU:0, one launch (start us, length us, event | category | flops | bytes accessed | tf_op | source)
XLA Modules:
  0.0 911.1 jit_solution(9728621388558323904)
XLA Ops:
  7.2 0.0 reduce-scatter.8.cloned.1.call-start
  7.2 6.5 copy.20
  13.7 3.1 fusion.9
  16.8 24.4 %fusion.30 = f32[2048,4096]{1,0:T(8,128)} fusion(bf16[2,1024,4096]{2,1,0:T(8,128)(2,1)} %param.13, bf16[1,2048,1024]{2,1,0:T(8,128)(2,1)} %param.11, f32[2048]{0:T(1024)S(1)} %add_rsqrt_fusion), kind=kOutput, calls=%fused_computation.47 | convolution fusion | flops 17186160640 | bytes 46145536 | tf_op jit(solution)/shard_map/dot_general | solution.py:16
  41.3 38.0 %multiply_convert_fusion.1 = (bf16[2048,4096]{1,0:T(8,128)(2,1)}, f32[2048,4096]{1,0:T(8,128)}) fusion(f32[2048,4096]{1,0:T(8,128)} %fusion.30, bf16[2,1024,4096]{2,1,0:T(8,128)(2,1)} %param.14, bf16[1,2048,1024]{2,1,0:T(8,128)(2,1)} %param.11, f32[2048]{0:T(1024)S(1)} %add_rsqrt_fusion), kind=kOutput, calls=%fused_computation.13 | convolution fusion | flops 17236492288 | bytes 96477184 | tf_op jit(solution)/shard_map/dot_general | solution.py:16
  79.2 23.7 %fusion.13 = (f32[2048]{0:T(1024)S(1)}, bf16[2048,1024]{0,1:T(8,128)(2,1)S(1)}) fusion(bf16[2048,4096]{1,0:T(8,128)(2,1)} %get-tuple-element.40, bf16[2,4096,1024]{2,1,0:T(8,128)(2,1)} %param.15, bf16[1,2048,1024]{1,2,0:T(8,128)(2,1)} %copy.20), kind=kOutput, calls=%fused_computation.30 | convolution fusion | flops 17190352896 | bytes 33562624 | tf_op jit(solution)/shard_map/dot_general | solution.py:16
  103.0 0.0 copy-start.2
  103.0 0.0 copy-start.16
  103.0 24.9 %fusion.19 = f32[2048,4096]{1,0:T(8,128)} fusion(bf16[2,1024,4096]{2,1,0:T(8,128)(2,1)} %param.14, bf16[2048,1024]{0,1:T(8,128)(2,1)S(1)} %get-tuple-element.43, f32[2048]{0:T(1024)S(1)} %fusion.69), kind=kOutput, calls=%fused_computation.36 | convolution fusion | flops 17186160640 | bytes 46145536 | tf_op jit(solution)/shard_map/dot_general | solution.py:16
  127.9 23.6 %fusion.23 = f32[2048,4096]{1,0:T(8,128)} fusion(bf16[2,1024,4096]{2,1,0:T(8,128)(2,1)} %param.13, bf16[2048,1024]{0,1:T(8,128)(2,1)S(1)} %get-tuple-element.43, f32[2048]{0:T(1024)S(1)} %fusion.69), kind=kOutput, calls=%fused_computation.40 | convolution fusion | flops 17186160640 | bytes 46145536 | tf_op jit(solution)/shard_map/dot_general | solution.py:16
  151.5 30.6 %fusion.35 = bf16[4096,1024]{1,0:T(8,128)(2,1)} fusion(f32[2048,4096]{1,0:T(8,128)} %fusion.19, f32[2048,4096]{1,0:T(8,128)} %fusion.23, bf16[1,2048,1024]{2,1,0:T(8,128)(2,1)} %param.12), kind=kOutput, calls=%fused_computation.53 | convolution fusion | flops 17234395136 | bytes 79691776 | tf_op jit(solution)/shard_map/dot_general | solution.py:16
  182.0 0.0 reduce-scatter.8.cloned.1.call-update
  182.0 0.0 reduce-scatter.6.cloned.1.call-start
  182.1 6.9 copy.21
  189.0 51.3 %fusion.2 = (bf16[2048,4096]{1,0:T(8,128)(2,1)}, bf16[2048,4096]{1,0:T(8,128)(2,1)}) fusion(f32[2048,4096]{1,0:T(8,128)} %fusion.23, f32[2048,4096]{1,0:T(8,128)} %fusion.19, bf16[2048,1024]{0,1:T(8,128)(2,1)} %bitcast.76, bf16[2,4096,1024]{2,1,0:T(8,128)(2,1)} %param.15), kind=kOutput, calls=%fused_computation.6 | convolution fusion | flops 17305698304 | bytes 113246208 | tf_op jit(solution)/shard_map/dot_general | solution.py:16
  240.4 21.8 %convolution_convert_fusion.3 = bf16[1024,4096]{1,0:T(8,128)(2,1)} fusion(bf16[2048,4096]{1,0:T(8,128)(2,1)} %get-tuple-element.20, bf16[2048,1024]{0,1:T(8,128)(2,1)S(1)} %copy-done.3, f32[2048]{0:T(1024)S(1)} %fusion.69), kind=kOutput, calls=%fused_computation.55 | convolution fusion | flops 17190354944 | bytes 29368320 | tf_op jit(solution)/shard_map/dot_general | solution.py:16
  262.1 0.0 reduce-scatter.6.cloned.1.call-update
  262.1 0.0 reduce-scatter.4.cloned.1.call-start
  262.2 23.0 %convolution_convert_fusion.4 = bf16[1024,4096]{1,0:T(8,128)(2,1)} fusion(bf16[2048,4096]{1,0:T(8,128)(2,1)} %get-tuple-element.19, bf16[2048,1024]{0,1:T(8,128)(2,1)} %copy-done.2, f32[2048]{0:T(1024)S(1)} %fusion.69), kind=kOutput, calls=%fused_computation.56 | convolution fusion | flops 17190354944 | bytes 29368320 | tf_op jit(solution)/shard_map/dot_general | solution.py:16
  285.2 0.0 reduce-scatter.4.cloned.1.call-update
  285.3 23.0 %fusion.17 = bf16[2048,1024]{0,1:T(8,128)(2,1)S(1)} fusion(bf16[2048,4096]{1,0:T(8,128)(2,1)} %get-tuple-element.20, bf16[2,1024,4096]{2,1,0:T(8,128)(2,1)} %param.14), kind=kOutput, calls=%fused_computation.34 | convolution fusion | flops 17179869184 | bytes 29360128 | tf_op jit(solution)/shard_map/dot_general | solution.py:16
  308.3 0.0 copy-start.17
  308.3 0.0 copy-start.15
  308.3 25.8 %fusion.15 = (f32[2048]{0:T(1024)S(1)}, bf16[2048,1024]{0,1:T(8,128)(2,1)}) fusion(bf16[2048,1024]{0,1:T(8,128)(2,1)S(1)} %copy-done.4, bf16[2048,1024]{0,1:T(8,128)(2,1)S(1)} %fusion.17, bf16[2048,4096]{1,0:T(8,128)(2,1)} %get-tuple-element.19, bf16[2,1024,4096]{2,1,0:T(8,128)(2,1)} %param.13), kind=kOutput, calls=%fused_computation.32 | convolution fusion | flops 17192450048 | bytes 37756928 | tf_op jit(solution)/shard_map/dot_general | solution.py:16
  334.2 5.7 fusion.45.refs_1_
  339.9 4.8 fusion.44
  344.7 23.1 %convolution_convert_fusion.2.refs_0_ = bf16[4096,1024]{1,0:T(8,128)(2,1)} fusion(bf16[2048,4096]{1,0:T(8,128)(2,1)} %get-tuple-element.40, bf16[2048,1024]{0,1:T(8,128)(2,1)S(1)} %fusion.44), kind=kOutput, calls=%fused_computation.54 | convolution fusion | flops 17184063488 | bytes 29360128 | tf_op jit(solution)/shard_map/dot_general | solution.py:16
  367.7 44.6 %fusion.5 = (bf16[2048,4096]{1,0:T(8,128)(2,1)}, bf16[2048,4096]{1,0:T(8,128)(2,1)}) fusion(f32[2048,4096]{1,0:T(8,128)} %fusion.30, f32[2048,4096]{1,0:T(8,128)} %get-tuple-element.41, bf16[2048,1024]{0,1:T(8,128)(2,1)S(1)} %fusion.44, bf16[2,4096,1024]{2,1,0:T(8,128)(2,1)} %param.15), kind=kOutput, calls=%fused_computation.9 | convolution fusion | flops 17305698304 | bytes 113246208 | tf_op jit(solution)/shard_map/dot_general | solution.py:16
  412.3 186.3 %last_gradients.1 = (bf16[256,1024]{1,0:T(8,128)(2,1)}, bf16[64,4096]{1,0:T(8,128)(2,1)}, bf16[64,4096]{1,0:T(8,128)(2,1)}) custom-call(bf16[4096,1024]{1,0:T(8,128)(2,1)} %convolution_convert_fusion.2.refs_0_, bf16[1024,2048]{1,0:T(8,128)(2,1)} %fusion.45.refs_1_, bf16[2048,4096]{1,0:T(8,128)(2,1)} %get-tuple-element.37.refs_2_, ...), custom_call_target="tpu_custom_call" | custom-call | tf_op jit(solution)/shard_map/last_gradients/pallas_call | solution.py:276
  598.6 0.0 copy-start.6
  598.6 0.0 reduce-scatter.8.cloned.1.call-done.refs_5_
  598.6 0.0 reduce-scatter.6.cloned.1.call-done.refs_3_
  598.7 0.0 reduce-scatter.4.cloned.1.call-done.refs_1_
  598.7 12.1 %sum_of_squares.1 = f32[8,128]{1,0:T(8,128)} custom-call(bf16[64,4096]{1,0:T(8,128)(2,1)} %get-tuple-element.21.refs_0_, bf16[64,4096]{1,0:T(8,128)(2,1)} %reduce-scatter.4.cloned.1.call-done.refs_1_, bf16[64,4096]{1,0:T(8,128)(2,1)} %get-tuple-element.22.refs_2_, bf16[64,4096]{1,0:T(8,128)(2,1)} %reduce-scatter.6.cloned.1.call-done.refs_3_, ...), custom_call_target="tpu_custom_call" | custom-call | tf_op jit(solution)/shard_map/sum_of_squares/pallas_call | solution.py:316
  610.8 0.0 copy-start.7
  610.8 0.0 copy-start.8
  610.8 0.0 copy-start.9
  610.8 1.3 slice.30
  613.5 6.0 fusion.63
  619.6 6.4 fusion.57
  626.0 244.3 %gather_weights.1 = (bf16[2,1024,4096]{2,1,0:T(8,128)(2,1)}, bf16[2,1024,4096]{2,1,0:T(8,128)(2,1)}, bf16[2,4096,1024]{2,1,0:T(8,128)(2,1)}) custom-call(bf16[2,64,4096]{2,1,0:T(8,128)(2,1)} %get-tuple-element.33.refs_0_, bf16[2,64,4096]{2,1,0:T(8,128)(2,1)} %get-tuple-element.46.refs_1_, bf16[2,256,1024]{2,1,0:T(8,128)(2,1)} %get-tuple-element.27.refs_2_), custom_call_target="tpu_custom_call" | custom-call | tf_op jit(solution)/shard_map/gather_weights/pallas_call | solution.py:123
  870.3 0.0 slice-start
  870.3 0.0 slice-start.1
  870.3 16.8 %copy.25 = bf16[2,1024,4096]{2,1,0:T(8,128)(2,1)} copy(bf16[2,1024,4096]{2,1,0:T(8,128)(2,1)} %get-tuple-element.58) | data formatting | bytes 33554432
  887.1 8.5 copy.26
  895.6 1.4 slice-done.2
  897.1 1.2 slice-done.3
  898.2 6.2 copy.27
  (36 shorter events, 0.1 us)
Async XLA Ops:
  7.2 591.4 %reduce-scatter.8.cloned.1.call-start = ((), (), s32[]{:S(2)}) async-start(), calls=%async_computation.5 | async-start | bytes 8912896 | tf_op jit(solution)/shard_map/reduce_scatter | solution.py:335
  16.8 24.5 %copy-start.14 = (f32[2048]{0:T(1024)}, f32[2048]{0:T(1024)S(1)}, u32[]{:S(2)}) copy-start(f32[2048]{0:T(1024)S(1)} %add_rsqrt_fusion) | copy-start | bytes 24580
  103.0 24.9 %copy-start.2 = (bf16[2048,1024]{0,1:T(8,128)(2,1)}, bf16[2048,1024]{0,1:T(8,128)(2,1)S(1)}, u32[]{:S(2)}) copy-start(bf16[2048,1024]{0,1:T(8,128)(2,1)S(1)} %get-tuple-element.43) | copy-start | bytes 12582916
  103.0 24.9 %copy-start.16 = (f32[2048]{0:T(1024)}, f32[2048]{0:T(1024)S(1)}, u32[]{:S(2)}) copy-start(f32[2048]{0:T(1024)S(1)} %get-tuple-element.42) | copy-start | bytes 24580
  182.0 416.6 %reduce-scatter.6.cloned.1.call-start = ((), (), s32[]{:S(2)}) async-start(), calls=%async_computation.4 | async-start | bytes 8912896 | tf_op jit(solution)/shard_map/reduce_scatter | solution.py:335
  189.0 51.3 %copy-start.3 = (bf16[2048,1024]{0,1:T(8,128)(2,1)S(1)}, bf16[2048,1024]{0,1:T(8,128)(2,1)}, u32[]{:S(2)}) copy-start(bf16[2048,1024]{0,1:T(8,128)(2,1)} %copy-done.2) | copy-start | bytes 12582916
  262.1 336.5 %reduce-scatter.4.cloned.1.call-start = ((), (), s32[]{:S(2)}) async-start(), calls=%async_computation.3 | async-start | bytes 8912896 | tf_op jit(solution)/shard_map/reduce_scatter | solution.py:335
  285.3 23.0 %copy-start.4 = (bf16[2048,1024]{0,1:T(8,128)(2,1)S(1)}, bf16[2048,1024]{0,1:T(8,128)(2,1)}, u32[]{:S(2)}) copy-start(bf16[2048,1024]{0,1:T(8,128)(2,1)} %copy-done.2) | copy-start | bytes 12582916
  308.3 25.8 %copy-start.17 = (f32[2048]{0:T(1024)S(1)}, f32[2048]{0:T(1024)}, u32[]{:S(2)}) copy-start(f32[2048]{0:T(1024)} %copy-done.16) | copy-start | bytes 24580
  308.3 25.8 %copy-start.15 = (f32[2048]{0:T(1024)S(1)}, f32[2048]{0:T(1024)}, u32[]{:S(2)}) copy-start(f32[2048]{0:T(1024)} %copy-done.14) | copy-start | bytes 24580
  334.2 5.7 copy-start
  334.2 5.7 copy-start.5
  598.6 21.0 %copy-start.6 = (f32[2,64,4096]{2,1,0:T(8,128)S(1)}, f32[2,64,4096]{2,1,0:T(8,128)}, u32[]{:S(2)}) copy-start(f32[2,64,4096]{2,1,0:T(8,128)} %param.19) | copy-start | bytes 6291460
  598.7 20.9 %copy-start.10 = (bf16[64,4096]{1,0:T(8,128)(2,1)S(1)}, bf16[64,4096]{1,0:T(8,128)(2,1)}, u32[]{:S(2)}) copy-start(bf16[64,4096]{1,0:T(8,128)(2,1)} %reduce-scatter.6.cloned.1.call-done.refs_3_) | copy-start | bytes 1572868
  598.7 20.9 %copy-start.11 = (bf16[64,4096]{1,0:T(8,128)(2,1)S(1)}, bf16[64,4096]{1,0:T(8,128)(2,1)}, u32[]{:S(2)}) copy-start(bf16[64,4096]{1,0:T(8,128)(2,1)} %reduce-scatter.4.cloned.1.call-done.refs_1_) | copy-start | bytes 1572868
  610.8 8.8 copy-start.7
  610.8 8.8 copy-start.8
  610.8 8.8 copy-start.9
  610.8 8.8 copy-start.12
  610.8 8.8 copy-start.13
  870.3 16.8 %copy-start.1 = (bf16[2,1024,4096]{2,1,0:T(8,128)(2,1)S(1)}, bf16[2,1024,4096]{2,1,0:T(8,128)(2,1)}, u32[]{:S(2)}) copy-start(bf16[2,1024,4096]{2,1,0:T(8,128)(2,1)} %get-tuple-element.59) | copy-start | bytes 50331652
  870.3 25.3 %slice-start = ((s8[16777216]{0:T(1024)(128)(4,1)}), s8[4194304]{0:T(1024)(128)(4,1)S(1)}, s32[]{:S(2)}) async-start(s8[16777216]{0:T(1024)(128)(4,1)} %bitcast.78), calls=%async_computation.6 | async-start | bytes 8388608
  870.3 25.3 %slice-start.1 = ((s8[16777216]{0:T(1024)(128)(4,1)}), s8[4194304]{0:T(1024)(128)(4,1)S(1)}, s32[]{:S(2)}) async-start(s8[16777216]{0:T(1024)(128)(4,1)} %bitcast.78), calls=%async_computation.7 | async-start | bytes 8388608
  887.1 9.9 %slice-start.2 = ((s8[16777216]{0:T(1024)(128)(4,1)}), s8[4194304]{0:T(1024)(128)(4,1)S(1)}, s32[]{:S(2)}) async-start(s8[16777216]{0:T(1024)(128)(4,1)} %bitcast.78), calls=%async_computation.8 | async-start | bytes 8388608
  887.1 11.1 %slice-start.3 = ((s8[16777216]{0:T(1024)(128)(4,1)}), s8[4194304]{0:T(1024)(128)(4,1)S(1)}, s32[]{:S(2)}) async-start(s8[16777216]{0:T(1024)(128)(4,1)} %bitcast.78), calls=%async_computation.9 | async-start | bytes 8388608
Sparse Core Ops, SparseCore 0:
  182.2 106.1 reduce-scatter.7
  292.4 103.0 reduce-scatter.5
  399.6 141.7 reduce-scatter.3

commit v4 on v3

--- a/solution.py
+++ b/solution.py
@@ -138,25 +138,29 @@
     return total
 
 
-def last_kernel(n, refs_in, refs_out, own, made, tiles, got, buf, sems):
-    down, a_t, *by_hidden = refs_in
-    own_sem, d2d_send, d2d_recv, ring_send, ring_recv, tile_sem = sems
-    chips, k = n // 2, 3
-    grads = (down, made.at[0], made.at[1])
+def last_kernel(n, refs_in, refs_out, total_ref, own, made, tiles, got, buf, slots, sems):
+    down, early, a_t, *by_hidden = refs_in[:5]
+    done = refs_in[5:]
+    own_sem, d2d_send, d2d_recv, ring_send, ring_recv, tile_sem, total_send, total_recv, credit = sems
+    chips, k = n // 2, 4
+    me = lax.axis_index("dp")
+    others = [(me + j) % n for j in range(1, n)]
+    grads = (down, made.at[0], made.at[1], early)
+    own, got, buf = {0: own[0], 3: own[1]}, (*got, got[2]), (*buf, buf[2])
     rows = [g.shape[0] // n for g in grads]
     wide = [g.shape[1] // 2 for g in grads]
     core, pos, owner = place(n)
     right, left = owner((pos + 1) % chips, core), owner((pos + chips - 1) % chips, core)
     partner = owner(pos, 1 - core)
-    entry_barrier((left, right, partner))
+    entry_barrier(others)
     to = (right, left)
 
     def start_row(i, d, c, more=0):
         at = owner((pos + d) % chips, c) * rows[i] + more
         return pl.multiple_of(at, rows[i] // 2)
 
-    def load(d):
-        return pltpu.make_async_copy(down.at[pl.ds(start_row(0, d, core), rows[0])], own.at[d], own_sem.at[d])
+    def load(i, d):
+        return pltpu.make_async_copy(grads[i].at[pl.ds(start_row(i, d, core), rows[i])], own[i].at[d], own_sem.at[i, d])
 
     def cross(i, d):
         src = grads[i].at[pl.ds(start_row(i, d, 1 - core), rows[i])]
@@ -177,8 +181,8 @@
     def begin(i):
         for d in order:
             cross(i, d).start()
-            if i == 0:
-                load(d).start()
+            if i in own:
+                load(i, d).start()
 
     ready = set()
 
@@ -189,13 +193,13 @@
             d = (chips - 1 - s if way == 0 else 1 + s) % chips
             if (i, d) not in ready:
                 ready.add((i, d))
-                if i == 0:
-                    load(d).wait()
+                if i in own:
+                    load(i, d).wait()
                 cross(i, d).wait_recv()
             if s > 0:
                 hop(i, part, way, s - 1).wait_recv()
             half = pl.ds(way * h, h)
-            mine = own.at[d, half] if i == 0 else grads[i].at[pl.ds(start_row(i, d, core, way * h), h)]
+            mine = own[i].at[d, half] if i in own else grads[i].at[pl.ds(start_row(i, d, core, way * h), h)]
             terms = [mine, got[i].at[d, half]] + ([buf[i].at[way, s]] if s > 0 else [])
             result = buf[i].at[way, s] if s < chips - 1 else refs_out[i].at[half]
 
@@ -216,7 +220,22 @@
         return pltpu.make_async_copy(src, tiles.at[t % 2], tile_sem.at[t % 2])
 
     high = min(512, a_t.shape[0])
+
+    def squares(refs):
+        total = jnp.zeros((8, 512), F32)
+        for ref in refs:
+            across = ref.shape[1] // 512
+
+            def add(c, total, ref=ref, across=across):
+                row = pl.multiple_of(c // across * 16, 16)
+                g = ref[pl.ds(row, 16), pl.ds(pl.multiple_of(c % across * 512, 512), 512)].astype(F32)
+                return total + g[:8] * g[:8] + g[8:] * g[8:]
+
+            total = lax.fori_loop(0, ref.shape[0] // 16 * across, add, total)
+        return total
+
     begin(0)
+    begin(3)
     fetch(0).start()
     gate, up = list(range(2 * chips)), list(range(2 * chips))
     for t in range(count):
@@ -234,94 +253,82 @@
         lax.fori_loop(0, a_t.shape[0] // high, matmul, 0)
         for number in range(t * 2 * chips // count, (t + 1) * 2 * chips // count):
             turn(0, number)
+            turn(3, number)
         if t == per - 1:
             begin(1)
-        if t > per:
-            turn(1, gate.pop(0))
+    for part in range(2):
+        for way in range(2):
+            for s in range(chips - 1):
+                hop(3, part, way, s).wait_send()
+    for d in (left, right, partner):
+        pl.semaphore_signal(credit, inc=1, device_id={"dp": d}, device_id_type=MESH)
+    turn(1, gate.pop(0))
+    turn(1, gate.pop(0))
+    pl.semaphore_wait(credit, 3)
     begin(2)
+    turn(1, gate.pop(0))
+    turn(1, gate.pop(0))
+    total = squares([refs_out[0], refs_out[3], *done])
     while gate or up:
         if gate:
             turn(1, gate.pop(0))
         if up:
             turn(2, up.pop(0))
+    total += squares(refs_out[1:3])
+    slots[0] = jnp.broadcast_to(jnp.sum(jnp.sum(total, 1, keepdims=True), 0, keepdims=True), (8, 128))
+    copies = [remote(slots.at[0], slots.at[j], total_send.at[j], total_recv.at[j], d) for j, d in enumerate(others, 1)]
+    for c in copies:
+        c.start()
     for i in range(k):
         for d in range(chips):
             cross(i, d).wait_send()
-        for part in range(2):
+        for part in range(2) if i < 3 else ():
             for way in range(2):
                 for s in range(chips - 1):
                     hop(i, part, way, s).wait_send()
-
-
-def last_gradients(n, down, a_t, by_gate, by_up, collective_id):
-    chips, k = n // 2, 3
-    shapes = [down.shape, (a_t.shape[0], by_gate.shape[1]), (a_t.shape[0], by_up.shape[1])]
-    rows = [s[0] // n for s in shapes]
-    dma = pltpu.SemaphoreType.DMA
-    scratch = (
-        [pltpu.VMEM((chips, rows[0], shapes[0][1]), BF16), pltpu.VMEM((2, *shapes[1]), BF16), pltpu.VMEM((2, a_t.shape[1], TILE), BF16)]
-        + [pltpu.VMEM((chips, r, s[1]), BF16) for r, s in zip(rows, shapes)]
-        + [pltpu.VMEM((2, chips, r // 2, s[1]), BF16) for r, s in zip(rows, shapes)]
-        + [dma((chips,))]
-        + [dma((k, chips))] * 2
-        + [dma((k, 2, 2, chips - 1))] * 2
-        + [dma((2,))]
-    )
-
-    def kernel(*refs):
-        own, made, tiles = refs[7:10]
-        last_kernel(n, refs[:4], refs[4:7], own, made, tiles, refs[10:13], refs[13:16], refs[16:])
-
-    hbm, vmem = pl.BlockSpec(memory_space=pl.ANY), pl.BlockSpec(memory_space=pltpu.VMEM)
-    return pl.pallas_call(
-        kernel,
-        out_shape=[jax.ShapeDtypeStruct((r, s[1]), BF16) for r, s in zip(rows, shapes)],
-        in_specs=[hbm, vmem, hbm, hbm],
-        out_specs=[vmem] * k,
-        scratch_shapes=scratch,
-        compiler_params=pltpu.CompilerParams(collective_id=collective_id, has_side_effects=True, vmem_limit_bytes=62 << 20),
-        name="last_gradients",
-    )(down, a_t, by_gate, by_up)
-
-
-def square_kernel(n, *refs):
-    ins, out, slots, send, recv = refs[:-4], refs[-4], refs[-3], refs[-2], refs[-1]
-    me = lax.axis_index("dp")
-    others = [(me + j) % n for j in range(1, n)]
-    entry_barrier(others)
-    total = jnp.zeros((8, 512), F32)
-    for ref in ins:
-        rows, cols = ref.shape
-
-        def add(c, total, ref=ref, cols=cols):
-            row = pl.multiple_of(c // (cols // 512) * 16, 16)
-            g = ref[pl.ds(row, 16), pl.ds(pl.multiple_of(c % (cols // 512) * 512, 512), 512)].astype(F32)
-            return total + g[:8] * g[:8] + g[8:] * g[8:]
-
-        total = lax.fori_loop(0, rows // 16 * (cols // 512), add, total)
-    slots[0] = jnp.broadcast_to(jnp.sum(jnp.sum(total, 1, keepdims=True), 0, keepdims=True), (8, 128))
-    copies = [remote(slots.at[0], slots.at[j], send.at[j], recv.at[j], d) for j, d in enumerate(others, 1)]
-    for c in copies:
-        c.start()
     for c in copies:
         c.wait_send()
         c.wait_recv()
     total = slots[0]
     for j in range(1, n):
         total += slots[j]
-    out[...] = total
-
-
-def sum_of_squares(n, blocks, collective_id):
+    total_ref[...] = total
+
+
+def last_gradients(n, down, early, a_t, by_gate, by_up, done, collective_id):
+    chips, k = n // 2, 4
+    shapes = [down.shape, (a_t.shape[0], by_gate.shape[1]), (a_t.shape[0], by_up.shape[1]), early.shape]
+    rows = [s[0] // n for s in shapes]
+    dma = pltpu.SemaphoreType.DMA
+    scratch = (
+        [pltpu.VMEM((chips, rows[i], shapes[i][1]), BF16) for i in (0, 3)]
+        + [pltpu.VMEM((2, *shapes[1]), BF16), pltpu.VMEM((2, a_t.shape[1], TILE), BF16)]
+        + [pltpu.VMEM((chips, r, s[1]), BF16) for r, s in zip(rows[:3], shapes)]
+        + [pltpu.VMEM((2, chips, r // 2, s[1]), BF16) for r, s in zip(rows[:3], shapes)]
+        + [pltpu.VMEM((n, 8, 128), F32)]
+        + [dma((k, chips))]
+        + [dma((k, chips))] * 2
+        + [dma((k, 2, 2, chips - 1))] * 2
+        + [dma((2,))]
+        + [dma((n,))] * 2
+        + [pltpu.SemaphoreType.REGULAR]
+    )
+    count = 5 + len(done)
+
+    def kernel(*refs):
+        ins, outs, total, refs = refs[:count], refs[count : count + k], refs[count + k], refs[count + k + 1 :]
+        last_kernel(n, ins, outs, total, refs[:2], refs[2], refs[3], refs[4:7], refs[7:10], refs[10], refs[11:])
+
+    hbm, vmem = pl.BlockSpec(memory_space=pl.ANY), pl.BlockSpec(memory_space=pltpu.VMEM)
     return pl.pallas_call(
-        functools.partial(square_kernel, n),
-        out_shape=jax.ShapeDtypeStruct((8, 128), F32),
-        in_specs=[pl.BlockSpec(memory_space=pltpu.VMEM)] * len(blocks),
-        out_specs=pl.BlockSpec(memory_space=pltpu.VMEM),
-        scratch_shapes=[pltpu.VMEM((n, 8, 128), F32)] + [pltpu.SemaphoreType.DMA((n,))] * 2,
-        compiler_params=pltpu.CompilerParams(collective_id=collective_id, has_side_effects=True),
-        name="sum_of_squares",
-    )(*blocks)[0, 0]
+        kernel,
+        out_shape=[jax.ShapeDtypeStruct((r, s[1]), BF16) for r, s in zip(rows, shapes)] + [jax.ShapeDtypeStruct((8, 128), F32)],
+        in_specs=[hbm, hbm, vmem, hbm, hbm] + [vmem] * len(done),
+        out_specs=[vmem] * (k + 1),
+        scratch_shapes=scratch,
+        compiler_params=pltpu.CompilerParams(collective_id=collective_id, has_side_effects=True, vmem_limit_bytes=62 << 20),
+        name="last_gradients",
+    )(down, early, a_t, by_gate, by_up, *done)
 
 
 def solution(mesh):
@@ -350,16 +357,15 @@
         t_gate1 = grad(a1, dg1)
         d_gate1 = scatter_by_xla(t_gate1)
         t_up1 = grad(a1, du1)
-        d_up1 = scatter_by_xla(t_up1)
         dg1, du1, _, _ = lax.optimization_barrier((dg1, du1, t_gate1, t_up1))
         da1 = dot(dg1, wg[1], 1, 1).astype(BF16) + dot(du1, wu[1], 1, 1).astype(BF16)
         dh1 = dy + norm_back(da1)[0]
         t_down0 = grad(hid0, dh1)
         dhid0 = dot(dh1, wd[0], 1, 1).astype(BF16)
         dg0, du0 = act_back(g0, u0, dhid0)
-        d_down0, d_gate0, d_up0 = last_gradients(n, t_down0, a0.T, dg0, du0, 1)
+        d_down0, d_gate0, d_up0, d_up1, total = last_gradients(n, t_down0, t_up1, a0.T, dg0, du0, (d_down1, d_gate1), 1)
         gs = [(d_gate0, d_gate1), (d_up0, d_up1), (d_down0, d_down1)]
-        total = sum_of_squares(n, [g for pair in gs for g in pair], 2)
+        total = total[0, 0]
         count = sum(w.size for w in (wg, wu, wd))
         factor = jnp.minimum(1.0, 0.5 * lax.rsqrt(total / count + 1e-30))
         me = lax.axis_index("dp")

time: 919 us -> 905 us (0.985)
  Pallas kernels: 443 us -> 429 us
    pallas_call x1 -> x0, Pallas kernels: 12.1 us -> none  [sum_of_squares(): pl.pallas_call(functools.partial(square_kernel, n), out_shape=jax.ShapeDt...]
    unnamed x49 -> x51, local copies, waits for them, and re-layouts: 47.6 us -> 47.6 us
  transfers between devices with their start and end apart: 3 -> 2, of which waited for: 0 -> 0; matrix products, arithmetic and copies ran while one was open for 25% -> 26% of each run, Pallas kernels for 20% -> 0%
where the time goes in v4:
time: 905 us; the launch traced here: 897 us
  Pallas kernels  429 us (47%)
  matrix products  377 us (42%)
  local copies, waits for them, and re-layouts  49 us (5%)
  other arithmetic  26.1 us (3%)
  between operations  15.9 us (2%)
    dot_general x13, matrix products, dot(): lax.dot_general(a, b, (((ca,), (cb,)), ((), ())), preferred_element_type=...  377 us
    pallas_call x1, Pallas kernels, gather(): pl.pallas_call(functools.partial(gather_kernel, n, rows), out_shape=[jax....  244 us
    pallas_call x1, Pallas kernels, last_gradients(): pl.pallas_call(kernel, out_shape=[jax.ShapeDtypeStruct((r, s[1]), BF16) f...  185 us
    unnamed x51, local copies, waits for them, and re-layouts  47.6 us
  transfers between devices with their start and end apart: 2, of which 0 were waited for; matrix products, arithmetic and copies ran while one was open for 26% of the time, Pallas kernels for 0%

profile of v4, /device:TPU:0, one launch (start us, length us, event | category | flops | bytes accessed | tf_op | source)
XLA Modules:
  0.0 897.0 jit_solution(6089579792854147935)
XLA Ops:
  7.2 0.0 reduce-scatter.3.cloned.1.call-start
  7.2 6.5 copy.20
  13.7 3.1 fusion.9
  16.8 0.0 copy-start.15
  16.8 24.3 %fusion.30 = f32[2048,4096]{1,0:T(8,128)} fusion(bf16[2,1024,4096]{2,1,0:T(8,128)(2,1)} %param.13, bf16[1,2048,1024]{2,1,0:T(8,128)(2,1)} %param.11, f32[2048]{0:T(1024)S(1)} %add_rsqrt_fusion), kind=kOutput, calls=%fused_computation.47 | convolution fusion | flops 17186160640 | bytes 46145536 | tf_op jit(solution)/shard_map/dot_general | solution.py:16
  41.2 0.0 copy-done.15
  41.2 38.0 %multiply_convert_fusion.1 = (bf16[2048,4096]{1,0:T(8,128)(2,1)}, f32[2048,4096]{1,0:T(8,128)}) fusion(f32[2048,4096]{1,0:T(8,128)} %fusion.30, bf16[2,1024,4096]{2,1,0:T(8,128)(2,1)} %param.14, bf16[1,2048,1024]{2,1,0:T(8,128)(2,1)} %param.11, f32[2048]{0:T(1024)S(1)} %add_rsqrt_fusion), kind=kOutput, calls=%fused_computation.13 | convolution fusion | flops 17236492288 | bytes 96477184 | tf_op jit(solution)/shard_map/dot_general | solution.py:16
  79.2 23.7 %fusion.13 = (f32[2048]{0:T(1024)S(1)}, bf16[2048,1024]{0,1:T(8,128)(2,1)S(1)}) fusion(bf16[2048,4096]{1,0:T(8,128)(2,1)} %get-tuple-element.44, bf16[2,4096,1024]{2,1,0:T(8,128)(2,1)} %param.15, bf16[1,2048,1024]{1,2,0:T(8,128)(2,1)} %copy.20), kind=kOutput, calls=%fused_computation.30 | convolution fusion | flops 17190352896 | bytes 33562624 | tf_op jit(solution)/shard_map/dot_general | solution.py:16
  102.9 0.0 copy-start.17
  102.9 24.7 %fusion.19 = f32[2048,4096]{1,0:T(8,128)} fusion(bf16[2,1024,4096]{2,1,0:T(8,128)(2,1)} %param.14, bf16[2048,1024]{0,1:T(8,128)(2,1)S(1)} %get-tuple-element.47, f32[2048]{0:T(1024)S(1)} %fusion.69), kind=kOutput, calls=%fused_computation.36 | convolution fusion | flops 17186160640 | bytes 46145536 | tf_op jit(solution)/shard_map/dot_general | solution.py:16
  127.7 0.0 copy-done.2
  127.7 23.4 %fusion.23 = f32[2048,4096]{1,0:T(8,128)} fusion(bf16[2,1024,4096]{2,1,0:T(8,128)(2,1)} %param.13, bf16[2048,1024]{0,1:T(8,128)(2,1)S(1)} %get-tuple-element.47, f32[2048]{0:T(1024)S(1)} %fusion.69), kind=kOutput, calls=%fused_computation.40 | convolution fusion | flops 17186160640 | bytes 46145536 | tf_op jit(solution)/shard_map/dot_general | solution.py:16
  151.1 30.6 %fusion.35 = bf16[4096,1024]{1,0:T(8,128)(2,1)} fusion(f32[2048,4096]{1,0:T(8,128)} %fusion.19, f32[2048,4096]{1,0:T(8,128)} %fusion.23, bf16[1,2048,1024]{2,1,0:T(8,128)(2,1)} %param.12), kind=kOutput, calls=%fused_computation.53 | convolution fusion | flops 17234395136 | bytes 79691776 | tf_op jit(solution)/shard_map/dot_general | solution.py:16
  181.7 0.0 reduce-scatter.3.cloned.1.call-update
  181.7 0.0 reduce-scatter.5.cloned.1.call-start
  181.7 7.0 copy.21
  188.7 51.3 %fusion.2 = (bf16[2048,4096]{1,0:T(8,128)(2,1)}, bf16[2048,4096]{1,0:T(8,128)(2,1)}) fusion(f32[2048,4096]{1,0:T(8,128)} %fusion.23, f32[2048,4096]{1,0:T(8,128)} %fusion.19, bf16[2048,1024]{0,1:T(8,128)(2,1)} %bitcast.76, bf16[2,4096,1024]{2,1,0:T(8,128)(2,1)} %param.15), kind=kOutput, calls=%fused_computation.6 | convolution fusion | flops 17305698304 | bytes 113246208 | tf_op jit(solution)/shard_map/dot_general | solution.py:16
  240.0 21.7 %convolution_convert_fusion.4 = bf16[1024,4096]{1,0:T(8,128)(2,1)} fusion(bf16[2048,4096]{1,0:T(8,128)(2,1)} %get-tuple-element.21, bf16[2048,1024]{0,1:T(8,128)(2,1)S(1)} %copy-done.3, f32[2048]{0:T(1024)S(1)} %fusion.69), kind=kOutput, calls=%fused_computation.56 | convolution fusion | flops 17190354944 | bytes 29368320 | tf_op jit(solution)/shard_map/dot_general | solution.py:16
  261.7 0.0 reduce-scatter.5.cloned.1.call-update
  261.8 22.9 %convolution_convert_fusion.3.refs_1_ = bf16[1024,4096]{1,0:T(8,128)(2,1)} fusion(bf16[2048,4096]{1,0:T(8,128)(2,1)} %get-tuple-element.22, bf16[2048,1024]{0,1:T(8,128)(2,1)} %copy-done.2, f32[2048]{0:T(1024)S(1)} %fusion.69), kind=kOutput, calls=%fused_computation.55 | convolution fusion | flops 17190354944 | bytes 29368320 | tf_op jit(solution)/shard_map/dot_general | solution.py:16
  284.6 23.2 %fusion.17 = bf16[2048,1024]{0,1:T(8,128)(2,1)S(1)} fusion(bf16[2048,4096]{1,0:T(8,128)(2,1)} %get-tuple-element.22, bf16[2,1024,4096]{2,1,0:T(8,128)(2,1)} %param.14), kind=kOutput, calls=%fused_computation.34 | convolution fusion | flops 17179869184 | bytes 29360128 | tf_op jit(solution)/shard_map/dot_general | solution.py:16
  307.8 0.0 copy-start.18
  307.8 0.0 copy-start.16
  307.8 25.6 %fusion.15 = (f32[2048]{0:T(1024)S(1)}, bf16[2048,1024]{0,1:T(8,128)(2,1)}) fusion(bf16[2048,1024]{0,1:T(8,128)(2,1)S(1)} %copy-done.4, bf16[2048,1024]{0,1:T(8,128)(2,1)S(1)} %fusion.17, bf16[2048,4096]{1,0:T(8,128)(2,1)} %get-tuple-element.21, bf16[2,1024,4096]{2,1,0:T(8,128)(2,1)} %param.13), kind=kOutput, calls=%fused_computation.32 | convolution fusion | flops 17192450048 | bytes 37756928 | tf_op jit(solution)/shard_map/dot_general | solution.py:16
  333.4 0.0 copy-done.18
  333.5 5.7 fusion.45.refs_2_
  339.2 0.0 copy-done.5
  339.2 4.8 fusion.44
  344.0 23.3 %convolution_convert_fusion.2.refs_0_ = bf16[4096,1024]{1,0:T(8,128)(2,1)} fusion(bf16[2048,4096]{1,0:T(8,128)(2,1)} %get-tuple-element.44, bf16[2048,1024]{0,1:T(8,128)(2,1)S(1)} %fusion.44), kind=kOutput, calls=%fused_computation.54 | convolution fusion | flops 17184063488 | bytes 29360128 | tf_op jit(solution)/shard_map/dot_general | solution.py:16
  367.3 44.2 %fusion.5 = (bf16[2048,4096]{1,0:T(8,128)(2,1)}, bf16[2048,4096]{1,0:T(8,128)(2,1)}) fusion(f32[2048,4096]{1,0:T(8,128)} %fusion.30, f32[2048,4096]{1,0:T(8,128)} %get-tuple-element.45, bf16[2048,1024]{0,1:T(8,128)(2,1)S(1)} %fusion.44, bf16[2,4096,1024]{2,1,0:T(8,128)(2,1)} %param.15), kind=kOutput, calls=%fused_computation.9 | convolution fusion | flops 17305698304 | bytes 113246208 | tf_op jit(solution)/shard_map/dot_general | solution.py:16
  411.5 184.7 %last_gradients.1 = (bf16[256,1024]{1,0:T(8,128)(2,1)}, bf16[64,4096]{1,0:T(8,128)(2,1)}, bf16[64,4096]{1,0:T(8,128)(2,1)}, bf16[64,4096]{1,0:T(8,128)(2,1)}, f32[8,128]{1,0:T(8,128)}) custom-call(bf16[4096,1024]{1,0:T(8,128)(2,1)} %convolution_convert_fusion.2.refs_0_, bf16[1024,4096]{1,0:T(8,128)(2,1)} %convolution_convert_fusion.3.refs_1_, ...), custom_call_target="tpu_custom_call" | custom-call | tf_op jit(solution)/shard_map/last_gradients/pallas_call | solution.py:323
  596.2 0.0 copy-start.8
  596.2 0.0 copy-start.9
  596.2 0.0 copy-start.10
  596.2 0.0 copy-start.11
  596.3 1.3 slice.30
  599.0 6.1 fusion.63
  605.1 0.0 copy-done.7
  605.2 6.4 fusion.57
  611.6 244.3 %gather_weights.1 = (bf16[2,1024,4096]{2,1,0:T(8,128)(2,1)}, bf16[2,1024,4096]{2,1,0:T(8,128)(2,1)}, bf16[2,4096,1024]{2,1,0:T(8,128)(2,1)}) custom-call(bf16[2,64,4096]{2,1,0:T(8,128)(2,1)} %get-tuple-element.37.refs_0_, bf16[2,64,4096]{2,1,0:T(8,128)(2,1)} %get-tuple-element.50.refs_1_, bf16[2,256,1024]{2,1,0:T(8,128)(2,1)} %get-tuple-element.31.refs_2_), custom_call_target="tpu_custom_call" | custom-call | tf_op jit(solution)/shard_map/gather_weights/pallas_call | solution.py:123
  855.9 0.0 slice-start
  855.9 0.0 slice-start.1
  855.9 16.8 %copy.25 = bf16[2,1024,4096]{2,1,0:T(8,128)(2,1)} copy(bf16[2,1024,4096]{2,1,0:T(8,128)(2,1)} %get-tuple-element.62) | data formatting | bytes 33554432
  872.7 0.0 copy-done.1
  872.7 8.5 copy.26
  881.2 1.4 slice-done.2
  882.6 1.2 slice-done.3
  883.8 6.2 copy.27
  (34 shorter events, 0.1 us)
Async XLA Ops:
  7.2 404.3 %reduce-scatter.3.cloned.1.call-start = ((), (), s32[]{:S(2)}) async-start(), calls=%async_computation.2 | async-start | bytes 8912896 | tf_op jit(solution)/shard_map/reduce_scatter | solution.py:342
  16.8 24.4 %copy-start.15 = (f32[2048]{0:T(1024)}, f32[2048]{0:T(1024)S(1)}, u32[]{:S(2)}) copy-start(f32[2048]{0:T(1024)S(1)} %add_rsqrt_fusion) | copy-start | bytes 24580
  102.9 24.8 %copy-start.2 = (bf16[2048,1024]{0,1:T(8,128)(2,1)}, bf16[2048,1024]{0,1:T(8,128)(2,1)S(1)}, u32[]{:S(2)}) copy-start(bf16[2048,1024]{0,1:T(8,128)(2,1)S(1)} %get-tuple-element.47) | copy-start | bytes 12582916
  102.9 24.8 %copy-start.17 = (f32[2048]{0:T(1024)}, f32[2048]{0:T(1024)S(1)}, u32[]{:S(2)}) copy-start(f32[2048]{0:T(1024)S(1)} %get-tuple-element.46) | copy-start | bytes 24580
  181.7 229.8 %reduce-scatter.5.cloned.1.call-start = ((), (), s32[]{:S(2)}) async-start(), calls=%async_computation.3 | async-start | bytes 8912896 | tf_op jit(solution)/shard_map/reduce_scatter | solution.py:342
  188.7 51.3 %copy-start.3 = (bf16[2048,1024]{0,1:T(8,128)(2,1)S(1)}, bf16[2048,1024]{0,1:T(8,128)(2,1)}, u32[]{:S(2)}) copy-start(bf16[2048,1024]{0,1:T(8,128)(2,1)} %copy-done.2) | copy-start | bytes 12582916
  284.6 23.2 %copy-start.4 = (bf16[2048,1024]{0,1:T(8,128)(2,1)S(1)}, bf16[2048,1024]{0,1:T(8,128)(2,1)}, u32[]{:S(2)}) copy-start(bf16[2048,1024]{0,1:T(8,128)(2,1)} %copy-done.2) | copy-start | bytes 12582916
  307.8 25.6 %copy-start.18 = (f32[2048]{0:T(1024)S(1)}, f32[2048]{0:T(1024)}, u32[]{:S(2)}) copy-start(f32[2048]{0:T(1024)} %copy-done.17) | copy-start | bytes 24580
  307.8 25.6 %copy-start.16 = (f32[2048]{0:T(1024)S(1)}, f32[2048]{0:T(1024)}, u32[]{:S(2)}) copy-start(f32[2048]{0:T(1024)} %copy-done.15) | copy-start | bytes 24580
  333.4 5.7 copy-start
  333.5 5.7 copy-start.5
  411.5 187.5 %copy-start.6 = (bf16[256,1024]{1,0:T(8,128)(2,1)S(1)}, bf16[256,1024]{1,0:T(8,128)(2,1)}, u32[]{:S(2)}) copy-start(bf16[256,1024]{1,0:T(8,128)(2,1)} %reduce-scatter.3.cloned.1.call-done.refs_5_) | copy-start | bytes 1572868
  596.2 8.9 copy-start.7
  596.2 8.9 copy-start.8
  596.2 8.9 copy-start.9
  596.2 8.9 copy-start.10
  596.2 8.9 copy-start.11
  596.3 8.9 copy-start.12
  596.3 8.9 copy-start.13
  596.3 8.9 copy-start.14
  855.9 16.8 %copy-start.1 = (bf16[2,1024,4096]{2,1,0:T(8,128)(2,1)S(1)}, bf16[2,1024,4096]{2,1,0:T(8,128)(2,1)}, u32[]{:S(2)}) copy-start(bf16[2,1024,4096]{2,1,0:T(8,128)(2,1)} %get-tuple-element.63) | copy-start | bytes 50331652
  855.9 25.3 %slice-start = ((s8[16777216]{0:T(1024)(128)(4,1)}), s8[4194304]{0:T(1024)(128)(4,1)S(1)}, s32[]{:S(2)}) async-start(s8[16777216]{0:T(1024)(128)(4,1)} %bitcast.78), calls=%async_computation.4 | async-start | bytes 8388608
  855.9 25.3 %slice-start.1 = ((s8[16777216]{0:T(1024)(128)(4,1)}), s8[4194304]{0:T(1024)(128)(4,1)S(1)}, s32[]{:S(2)}) async-start(s8[16777216]{0:T(1024)(128)(4,1)} %bitcast.78), calls=%async_computation.5 | async-start | bytes 8388608
  872.7 9.9 %slice-start.2 = ((s8[16777216]{0:T(1024)(128)(4,1)}), s8[4194304]{0:T(1024)(128)(4,1)S(1)}, s32[]{:S(2)}) async-start(s8[16777216]{0:T(1024)(128)(4,1)} %bitcast.78), calls=%async_computation.6 | async-start | bytes 8388608
  872.7 11.1 %slice-start.3 = ((s8[16777216]{0:T(1024)(128)(4,1)}), s8[4194304]{0:T(1024)(128)(4,1)S(1)}, s32[]{:S(2)}) async-start(s8[16777216]{0:T(1024)(128)(4,1)} %bitcast.78), calls=%async_computation.7 | async-start | bytes 8388608
Sparse Core Ops, SparseCore 0:
  181.8 106.1 reduce-scatter.2
  292.1 103.0 reduce-scatter.4
